TPU v7x, 32 devices: a whole 2x2x4 slice. The times are simulated.
32 devices in a mesh: seq: 8 (over z, y), head: 4 (over x, core).
Axes of the slice: x: 2, y: 2, z: 4, core: 2. Of those that a mesh axis runs over, the one named last changes fastest.
Arguments:
- queries: bfloat16 [2048, 4096], P('seq', 'head'), may hold values from -8 to 8
- self_keys: bfloat16 [2048, 1024], P('seq', 'head'), may hold values from -6 to 6
- self_values: bfloat16 [2048, 1024], P('seq', 'head'), may hold values from -6 to 6
- store_keys: bfloat16 [32768, 1024], P('seq', 'head'), may hold values from -6 to 6
- store_values: bfloat16 [32768, 1024], P('seq', 'head'), may hold values from -6 to 6
- kv_slot: int32 [256], replicated, may hold values from 0 to 255, as said below
- neighbours: int32 [16, 64], P('seq'), may hold values from 0 to 255, as said below
- counts: int32 [16], P('seq'), may hold values from 1 to 64, 96 in all
- out_weight: bfloat16 [4096, 4096], P('head', 'seq'), may hold values from -0.375 to 0.375
Outputs:
- mixed: bfloat16 [2048, 4096], P(('seq', 'head'))
Inputs may be any that keep to these rules, and one draw needn't show every extreme that they name: A permutation of the store blocks: block b is stored at slot kv_slot[b], on index kv_slot[b] // 32 of seq. `neighbours`: each row names 64 different store blocks in no particular order; only entries e < counts of the row are listed, the rest is padding. Counting by the index of seq on which a block is stored, each row names exactly 8 blocks on every index, and the 2 rows of one index of seq name the same single block on every index of seq.
All inputs are finite; a program needn't handle non-finite values. No bound on the sum of `counts` on one device may be relied on, other than what follows from the above.
Results may differ from a plain program's by a relative error of at most 0.012.
Values may be sent and summed in bfloat16 or wider, within the bound.
A program may use at most 128 MiB of HBM per device.

v0:
```python
import functools

import jax
import jax.numpy as jnp
from jax import lax
from jax.experimental import pallas as pl
from jax.experimental.pallas import tpu as pltpu
from jax.sharding import PartitionSpec as P

H = 32
KVH = 8
DH = 128
BLK = 128
NEG = -1e30
STAT = 8
SCAN = 4
LOG2E = 1.4426950408889634
MESH = pl.DeviceIdType.MESH


def asked_rows(q_ref, first_row, g, per_group):
    return jnp.concatenate(
        [
            q_ref[pl.ds(first_row, BLK), (g * per_group + r) * DH : (g * per_group + r + 1) * DH]
            for r in range(per_group)
        ],
        axis=0,
    )


def scores_of(keys, asked):
    scaling = DH ** (-0.5) * LOG2E
    return lax.dot_general(keys, asked, (((1,), (1,)), ((), ())), preferred_element_type=jnp.float32) * scaling


def weighed(values, p):
    return lax.dot_general(
        values, p.astype(jnp.bfloat16), (((0,), (0,)), ((), ())), preferred_element_type=jnp.float32
    )


def causal_mask(rows):
    position = lax.rem(lax.broadcasted_iota(jnp.int32, (BLK, rows), 1), BLK)
    return position >= lax.broadcasted_iota(jnp.int32, (BLK, rows), 0)


def write_part(o_ref, lse_ref, here, g, acc, total, lse):
    per_group = lse.shape[1] // BLK
    o_ref[here, g] = (acc * (1.0 / total)).astype(jnp.bfloat16)
    for r in range(STAT):
        at = (r % per_group) * BLK
        lse_ref[here, g, r : r + 1] = lse[:, at : at + BLK]


def part_row(
    block,
    here,
    first_row,
    done,
    local_blocks,
    store_blocks,
    slot_ref,
    near_ref,
    count_ref,
    q_ref,
    sk_ref,
    sv_ref,
    k_ref,
    v_ref,
    o_ref,
    lse_ref,
    list_ref,
    acc_ref,
    max_ref,
    sum_ref,
):
    owner, inner = lax.div(block, local_blocks), lax.rem(block, local_blocks)
    me = lax.axis_index("seq")
    per_group = H // KVH
    kv_here = k_ref.shape[1] // DH
    rows = per_group * BLK
    listed = count_ref[owner, 0, inner]
    first_slot = me * store_blocks

    def scan_entries(i, found):
        places = [slot_ref[near_ref[owner, inner, i * SCAN + u]] - first_slot for u in range(SCAN)]
        for u, place in enumerate(places):
            list_ref[found] = place
            kept = (place >= 0) & (place < store_blocks) & (i * SCAN + u < listed)
            found = found + kept.astype(jnp.int32)
        return found

    found = lax.fori_loop(0, lax.div(listed + (SCAN - 1), SCAN), scan_entries, jnp.int32(0))
    home = owner == me
    if not done:

        @pl.when(jnp.logical_and(found == 0, jnp.logical_not(home)))
        def _():
            o_ref[here] = jnp.zeros(o_ref.shape[1:], o_ref.dtype)
            lse_ref[here] = jnp.full(lse_ref.shape[1:], NEG, lse_ref.dtype)

    @pl.when(found > done if done else jnp.logical_or(found > 0, home))
    def _():
        if done:
            for g in range(kv_here):
                max_ref[g : g + 1] = jnp.concatenate(
                    [lse_ref[here, g, r : r + 1] for r in range(per_group)], axis=1
                )
                sum_ref[g : g + 1] = jnp.ones((1, rows), jnp.float32)
                acc_ref[g] = o_ref[here, g].astype(jnp.float32)
        else:

            @pl.when(home)
            def _():
                start = pl.multiple_of(inner * BLK, BLK)
                for g in range(kv_here):
                    cols = slice(g * DH, (g + 1) * DH)
                    asked = asked_rows(q_ref, first_row, g, per_group)
                    s = jnp.where(causal_mask(rows), scores_of(sk_ref[pl.ds(start, BLK), cols], asked), NEG)
                    m = jnp.max(s, axis=0, keepdims=True)
                    p = jnp.exp2(s - m)
                    max_ref[g : g + 1] = m
                    sum_ref[g : g + 1] = jnp.sum(p, axis=0, keepdims=True)
                    acc_ref[g] = weighed(sv_ref[pl.ds(start, BLK), cols], p)

            @pl.when(jnp.logical_not(home))
            def _():
                max_ref[...] = jnp.full_like(max_ref, NEG)
                sum_ref[...] = jnp.zeros_like(sum_ref)
                acc_ref[...] = jnp.zeros_like(acc_ref)

        def take(*places):
            starts = [pl.multiple_of(place * BLK, BLK) for place in places]

            def rows_of(ref, cols):
                return jnp.concatenate([ref[pl.ds(start, BLK), cols] for start in starts], axis=0)

            for g in range(kv_here):
                cols = slice(g * DH, (g + 1) * DH)
                s = scores_of(rows_of(k_ref, cols), asked_rows(q_ref, first_row, g, per_group))
                old = max_ref[g : g + 1]
                new = jnp.maximum(old, jnp.max(s, axis=0, keepdims=True))
                p = jnp.exp2(s - new)
                shrink = jnp.exp2(old - new)
                max_ref[g : g + 1] = new
                sum_ref[g : g + 1] = sum_ref[g : g + 1] * shrink + jnp.sum(p, axis=0, keepdims=True)
                acc_ref[g] = acc_ref[g] * shrink + weighed(rows_of(v_ref, cols), p)

        left = found - done

        @pl.loop(0, lax.div(left, 2))
        def _(i):
            take(list_ref[done + 2 * i], list_ref[done + 2 * i + 1])

        @pl.when(lax.rem(left, 2) == 1)
        def _():
            take(list_ref[found - 1])

        for g in range(kv_here):
            total = sum_ref[g : g + 1]
            write_part(o_ref, lse_ref, here, g, acc_ref[g], total, max_ref[g : g + 1] + jnp.log2(total))


def part_kernel(local_blocks, store_blocks, *refs):
    block = pl.program_id(0)
    part_row(block, 0, 0, 0, local_blocks, store_blocks, *refs)


def rest_kernel(local_blocks, store_blocks, *refs):
    def row(block, carry):
        first_row = pl.multiple_of(block * BLK, BLK)
        part_row(block, block, first_row, 1, local_blocks, store_blocks, *refs[:8], *refs[10:])
        return carry

    lax.fori_loop(0, refs[10].shape[0], row, 0)


def grant(*arrays):
    size = 0
    for shape, dtype in arrays:
        cells = 1
        for d in shape:
            cells = cells * d
        size += cells * jnp.dtype(dtype).itemsize
    return min(size + (4 << 20), 60 << 20)


def long_cost():
    return pl.CostEstimate(flops=200_000_000_000, bytes_accessed=1 << 20, transcendentals=0)


def ring_place(index, n):
    odd = lax.rem(index, 2)
    half = index // 2
    return (1 - odd) * half + odd * (n - 1 - half)


def ring_index(place, n):
    place = lax.rem(place + 2 * n, n)
    far = place // (n // 2)
    return (1 - far) * (2 * place) + far * (2 * (n - 1 - place) + 1)


def gather_kernel(n, pieces, early, *refs):
    refs = list(refs)

    def some(count):
        return [refs.pop(0) for _ in range(count)]

    x_ref, near_ref, count_ref = some(3)
    if early:
        slot_hbm, *store_hbm = some(5)
    out_ref, nears_ref, counts_ref = some(3)
    if early:
        o_ref, lse_ref, slot_ref, near_smem, count_smem, sk_ref, sv_ref, k_ref, v_ref, load_sem = some(10)
    own_sem, send_sem, recv_sem, tsend_sem, trecv_sem = refs
    me = lax.axis_index("seq")
    place = ring_place(me, n)
    rows = x_ref.shape[0]
    sub = rows // pieces
    half = n // 2
    ways = (1, -1)
    beside = [ring_index(place + way, n) for way in ways]
    own = [
        pltpu.make_async_copy(source, target, own_sem.at[i])
        for i, (source, target) in enumerate(
            (
                (x_ref, out_ref.at[pl.ds(pl.multiple_of(me * rows, rows), rows)]),
                (near_ref, nears_ref.at[me]),
                (count_ref, counts_ref.at[me]),
            )
        )
    ]
    for one in own:
        one.start()
    loads = []
    if early:
        sources = [slot_hbm] + store_hbm
        for i, (source, target) in enumerate(zip(sources, (slot_ref, sk_ref, sv_ref, k_ref, v_ref))):
            loads.append(pltpu.make_async_copy(source, target, load_sem.at[i]))
    for one in loads:
        one.start()
    barrier = pltpu.get_barrier_semaphore()
    for k in range(1, n):
        pl.semaphore_signal(barrier, inc=1, device_id={"seq": lax.rem(me + k, n)}, device_id_type=MESH)
    for one in own:
        one.wait()
    pl.semaphore_wait(barrier, n - 1)

    def copy(way, step, piece):
        owner = ring_index(place - ways[way] * step, n)
        there = pl.ds(pl.multiple_of(owner * rows + piece * sub, sub), sub)
        return pltpu.make_async_remote_copy(
            src_ref=out_ref.at[there],
            dst_ref=out_ref.at[there],
            send_sem=send_sem.at[way, step, piece],
            recv_sem=recv_sem.at[way, step, piece],
            device_id={"seq": beside[way]},
            device_id_type=MESH,
        )

    def piece_of(way, spot):
        return spot if way == 0 else pieces - 1 - spot

    started = []
    for spot in range(pieces):
        for way in range(2):
            one = copy(way, 0, piece_of(way, spot))
            one.start()
            started.append(one)
    table_copies = []
    for t, target in enumerate((nears_ref, counts_ref)):
        for k in range(1, n):
            table_copies.append(
                pltpu.make_async_remote_copy(
                    src_ref=target.at[me],
                    dst_ref=target.at[me],
                    send_sem=tsend_sem.at[t, k],
                    recv_sem=trecv_sem.at[t, k],
                    device_id={"seq": lax.rem(me + k, n)},
                    device_id_type=MESH,
                )
            )
    for one in table_copies:
        one.start()

    def first_listed(owner, inner):
        degree = near_ref.shape[1]
        store_blocks = k_ref.shape[0]
        listed = count_smem[owner, 0, inner]

        def look(i, best):
            e = degree - SCAN * (i + 1)
            for u in range(SCAN - 1, -1, -1):
                spot = slot_ref[near_smem[owner, inner, e + u]] - me * store_blocks
                kept = ((spot >= 0) & (spot < store_blocks) & (e + u < listed)).astype(jnp.int32)
                best = best + kept * (spot - best)
            return best

        return lax.fori_loop(0, degree // SCAN, look, jnp.int32(-1))

    def row_work(owner, inner, mine):
        per_group = H // KVH
        spot = first_listed(owner, inner)
        taken = jnp.maximum(spot, 0)
        missing = jnp.minimum(spot, 0).astype(jnp.float32) * -NEG
        first_row = pl.multiple_of(owner * rows + inner * BLK, BLK)
        for g in range(k_ref.shape[2] // DH):
            cols = slice(g * DH, (g + 1) * DH)
            asked = asked_rows(out_ref, first_row, g, per_group)
            keys, values = k_ref[taken, :, cols], v_ref[taken, :, cols]
            if mine:
                near = pl.ds(pl.multiple_of(inner * BLK, BLK), BLK)
                keys = jnp.concatenate([sk_ref[near, cols], keys], axis=0)
                values = jnp.concatenate([sv_ref[near, cols], values], axis=0)
            s = scores_of(keys, asked)
            if mine:
                inside = jnp.where(causal_mask(s.shape[1]), s[:BLK], NEG)
                s = jnp.concatenate([inside, s[BLK:] + missing], axis=0)
            m = jnp.max(s, axis=0, keepdims=True)
            p = jnp.exp2(s - m)
            total = jnp.sum(p, axis=0, keepdims=True)
            lse = m + jnp.log2(total)
            if not mine:
                lse = lse + missing
            write_part(o_ref, lse_ref, owner * pieces + inner, g, weighed(values, p), total, lse)

    def arrived(step, spot):
        if not early:
            return

        def one(way, carry):
            owner = ring_index(place - (1 - 2 * way) * step, n)
            row_work(owner, spot + way * (pieces - 1 - 2 * spot), False)
            return carry

        lax.fori_loop(0, 2, one, 0)

    if early:
        for one in table_copies:
            one.wait_recv()
        tables = [
            pltpu.make_async_copy(source, target, load_sem.at[5 + i])
            for i, (source, target) in enumerate(((nears_ref, near_smem), (counts_ref, count_smem)))
        ]
        for one in tables:
            one.start()
        for one in loads + tables:
            one.wait()
        lax.fori_loop(0, pieces, lambda inner, carry: (row_work(me, inner, True), carry)[1], 0)
    for step in range(1, half):
        for spot in range(pieces):
            for way in range(2):
                copy(way, step - 1, piece_of(way, spot)).wait_recv()
                if step < half - 1 or spot < pieces // 2:
                    one = copy(way, step, piece_of(way, spot))
                    one.start()
                    started.append(one)
            arrived(step, spot)
    for spot in range(pieces // 2):
        for way in range(2):
            copy(way, half - 1, piece_of(way, spot)).wait_recv()
        arrived(half, spot)
    for one in started:
        one.wait_send()
    for one in table_copies:
        if early:
            one.wait_send()
        else:
            one.wait()


def gathered(x, near, count, n, early):
    rows, width = x.shape
    pieces = rows // BLK
    vmem = pl.BlockSpec(memory_space=pltpu.VMEM)
    dma = pltpu.SemaphoreType.DMA
    kind = pltpu.VMEM if early else jax.ShapeDtypeStruct
    inputs = [x, near, count] + list(early)
    out_shape = [
        kind((n * rows, width), x.dtype),
        jax.ShapeDtypeStruct((n,) + near.shape, near.dtype),
        jax.ShapeDtypeStruct((n,) + count.shape, count.dtype),
    ]
    scratch = []
    held = [((n + 1, rows, width), x.dtype)]
    if early:
        slot, *stores = early
        kv_here = stores[2].shape[2] // DH
        part_shape = (n * pieces, kv_here, BLK, (H // KVH) * DH)
        out_shape += [kind(part_shape, x.dtype), kind((n * pieces, kv_here, STAT, BLK), jnp.float32)]
        scratch += [pltpu.SMEM(slot.shape, slot.dtype)]
        scratch += [pltpu.SMEM(out_shape[1].shape, near.dtype), pltpu.SMEM(out_shape[2].shape, count.dtype)]
        scratch += [pltpu.VMEM(a.shape, a.dtype) for a in stores]
        scratch += [dma((7,))]
        held += [(part_shape, x.dtype)] + [(a.shape, a.dtype) for a in stores]
    scratch += [
        dma((3,)),
        dma((2, n // 2, pieces)),
        dma((2, n // 2, pieces)),
        dma((2, n)),
        dma((2, n)),
    ]
    return pl.pallas_call(
        functools.partial(gather_kernel, n, pieces, bool(early)),
        in_specs=[pl.BlockSpec(memory_space=pltpu.HBM)] * len(inputs),
        out_specs=[vmem] * len(out_shape),
        out_shape=out_shape,
        scratch_shapes=scratch,
        compiler_params=pltpu.CompilerParams(
            collective_id=0,
            has_side_effects=True,
            vmem_limit_bytes=grant(*held),
        ),
        cost_estimate=long_cost(),
    )(*(pltpu.with_memory_space_constraint(a, pltpu.HBM) for a in inputs))


def merge(lse_a, lse_b):
    top = jnp.maximum(lse_a, lse_b)
    a = jnp.exp2(lse_a - top)
    b = jnp.exp2(lse_b - top)
    total = a + b
    return a / total, b / total, top + jnp.log2(total)


def reduce_kernel(
    n,
    small,
    o_ref,
    lse_ref,
    out_ref,
    got,
    got_lse,
    own,
    own_sem,
    send_sem,
    recv_sem,
    lsend_sem,
    lrecv_sem,
    ready=None,
):
    me = lax.axis_index("seq")
    place = ring_place(me, n)
    groups, width = got.shape[2], got.shape[4]
    ways = (1, -1)
    beside = [ring_index(place + way, n) for way in ways]
    if ready is None:
        barrier = pltpu.get_barrier_semaphore()
        for other in beside:
            pl.semaphore_signal(barrier, inc=1, device_id={"seq": other}, device_id_type=MESH)

    def home(way, step):
        return ring_index(place - ways[way] * (1 + step), n)

    def fetch(way, step):
        return pltpu.make_async_copy(
            o_ref.at[home(way, step) * 2 + way], own.at[way, lax.rem(step, 2)], own_sem.at[way, lax.rem(step, 2)]
        )

    def copies(way, step, g, before):
        at = home(way, step) * 2 + way
        first = before is None
        return (
            pltpu.make_async_remote_copy(
                src_ref=lse_ref.at[at, g] if first else got_lse.at[way, before, g],
                dst_ref=got_lse.at[way, step, g],
                send_sem=lsend_sem.at[way, step, g],
                recv_sem=lrecv_sem.at[way, step, g],
                device_id={"seq": beside[way]},
                device_id_type=MESH,
            ),
            pltpu.make_async_remote_copy(
                src_ref=o_ref.at[at, g] if first else got.at[way, before, g],
                dst_ref=got.at[way, step, g],
                send_sem=send_sem.at[way, step, g],
                recv_sem=recv_sem.at[way, step, g],
                device_id={"seq": beside[way]},
                device_id_type=MESH,
            ),
        )

    def merged(way, step, g):
        for one in copies(way, step - 1, g, step - 1):
            one.wait_recv()
        if g == 0 and not small:
            fetch(way, step).wait()
        at = home(way, step) * 2 + way
        theirs, ours, lse = merge(got_lse[way, step - 1, g], lse_ref[at, g])
        columns = []
        for r in range(width // DH):
            cols = slice(r * DH, (r + 1) * DH)
            mine = o_ref[at, g, :, cols] if small else own[way, lax.rem(step, 2), g, :, cols]
            columns.append(
                got[way, step - 1, g, :, cols].astype(jnp.float32) * theirs[r : r + 1]
                + mine.astype(jnp.float32) * ours[r : r + 1]
            )
        return columns, lse

    if not small:
        for way in range(2):
            fetch(way, 1).start()
    if ready is None:
        pl.semaphore_wait(barrier, 2)
    for g in range(groups):
        for way in range(2):
            for one in copies(way, 0, g, None):
                one.start()

    def one_step(step, carry):
        if not small:
            for way in range(2):
                fetch(way, step + 1).start()
        for g in range(groups):
            for way in range(2):
                columns, lse = merged(way, step, g)
                got_lse[way, step - 1, g] = lse
                for r, value in enumerate(columns):
                    got[way, step - 1, g, :, r * DH : (r + 1) * DH] = value.astype(jnp.bfloat16)
                for one in copies(way, step, g, step - 1):
                    one.start()
        return carry

    lax.fori_loop(1, n - 1, one_step, 0)
    for way in range(2):
        for g in range(groups):
            columns, _ = merged(way, n - 1, g)
            for r, value in enumerate(columns):
                at = g * width + r * DH
                out_ref[way * BLK : (way + 1) * BLK, at : at + DH] = jnp.transpose(value).astype(jnp.bfloat16)
        if ready is not None:
            ready(way)

    def drain_all():
        for g in range(groups):
            for way in range(2):
                for one in copies(way, 0, g, None):
                    one.wait_send()

        def drain(step, carry):
            for g in range(groups):
                for way in range(2):
                    for one in copies(way, step, g, step - 1):
                        one.wait_send()
            return carry

        lax.fori_loop(1, n - 1, drain, 0)

    if ready is None:
        drain_all()
    return drain_all


def project_stages(
    n,
    heads,
    x_ref,
    w_hbm,
    out_ref,
    w_ref,
    blocks,
    split,
    got,
    summed,
    landed,
    w_sem,
    wsend,
    wrecv,
    send_sem,
    recv_sem,
    hsend,
    hrecv,
    fsend,
    frecv,
):
    me = lax.axis_index("seq")
    mine = lax.axis_index("head")
    line = n // 2
    at, side = me // 2, lax.rem(me, 2)
    share = x_ref.shape[0] // heads
    columns = w_ref.shape[2]
    ways = (1, -1)
    early = min(2, line - 1)
    weights = pltpu.make_async_copy(w_hbm, w_ref.at[0], w_sem.at[0])
    weights.start()
    barrier = pltpu.get_barrier_semaphore()
    place = ring_place(me, n)
    for way in ways:
        other = ring_index(place + way, n)
        pl.semaphore_signal(barrier, inc=1, device_id={"seq": other}, device_id_type=MESH)
    for k in range(1, heads):
        pl.semaphore_signal(barrier, inc=1, device_id={"head": lax.rem(mine + k, heads)}, device_id_type=MESH)
    for k in range(1, line):
        other = lax.rem(at + k, line) * 2 + side
        pl.semaphore_signal(barrier, inc=1, device_id={"seq": other}, device_id_type=MESH)
    partner = at * 2 + 1 - side
    pl.semaphore_signal(barrier, inc=1, device_id={"seq": partner}, device_id_type=MESH)
    pl.semaphore_wait(barrier, heads + line + 1)

    def inside(spot):
        return jnp.logical_and(spot >= 0, spot < line)

    def copy(way, step, piece, first):
        there = (at - ways[way] * step, pl.ds(pl.multiple_of(piece * share, share), share))
        return pltpu.make_async_remote_copy(
            src_ref=x_ref.at[there[1]] if first else blocks.at[there],
            dst_ref=blocks.at[there],
            send_sem=send_sem.at[way, step, piece],
            recv_sem=recv_sem.at[way, step, piece],
            device_id={"seq": (at + ways[way]) * 2 + side},
            device_id_type=MESH,
        )

    def leaves(way, step):
        return jnp.logical_and(inside(at - ways[way] * step), inside(at + ways[way]))

    def to_head(i, j, source, to):
        return pltpu.make_async_remote_copy(
            src_ref=split.at[i, j, to],
            dst_ref=got.at[i, j, source],
            send_sem=hsend.at[i, j, to],
            recv_sem=hrecv.at[i, j, source],
            device_id={"head": to},
            device_id_type=MESH,
        )

    def to_row(i, j, source):
        owner = source * 2 + (side if j == 0 else 1 - side)
        return pltpu.make_async_remote_copy(
            src_ref=summed.at[i, j],
            dst_ref=landed.at[owner],
            send_sem=fsend.at[i, j],
            recv_sem=frecv.at[source, j],
            device_id={"seq": i * 2 + side},
            device_id_type=MESH,
        )

    def unit(i, c, js, own):
        rows = pl.ds(pl.multiple_of(c * share, share), share)
        value = x_ref[rows] if own else blocks[i, rows]
        for j in js:
            split[i, j, c] = jnp.dot(value, w_ref[j], preferred_element_type=jnp.float32).astype(jnp.bfloat16)

            @pl.when(mine != c)
            def _():
                to_head(i, j, mine, c).start()

    def visit(step, c, js, arriving):
        for way in range(2):
            i = at - ways[way] * step

            @pl.when(inside(i))
            def _():
                if arriving:
                    copy(way, step - 1, c, False).wait_recv()

                    @pl.when(inside(at + ways[way]))
                    def _():
                        copy(way, step, c, False).start()

                unit(i, c, js, False)

    def total_of(i, j):
        total = split[i, j, mine].astype(jnp.float32)
        for k in range(1, heads):
            source = lax.rem(mine + k, heads)
            to_head(i, j, source, mine).wait_recv()
            total = total + got[i, j, source].astype(jnp.float32)
        return total.astype(jnp.bfloat16)

    def settle_own(j):
        landed[at * 2 + (side if j == 0 else 1 - side)] = total_of(at, j)

    def settle(step, js):
        for way in range(2):
            i = at - ways[way] * step

            @pl.when(inside(i))
            def _():
                for j in js:
                    summed[i, j] = total_of(i, j)
                    to_row(i, j, at).start()

    def each(function):
        lax.fori_loop(0, heads, lambda c, carry: (function(c), carry)[1], 0)

    def start_own(c):
        for way in range(2):

            @pl.when(inside(at + ways[way]))
            def _():
                copy(way, 0, c, True).start()

    def run():
        weights.wait()
        exchange = pltpu.make_async_remote_copy(
            src_ref=w_ref.at[0],
            dst_ref=w_ref.at[1],
            send_sem=wsend.at[0],
            recv_sem=wrecv.at[0],
            device_id={"seq": partner},
            device_id_type=MESH,
        )
        exchange.start()
        each(lambda c: unit(at, c, (0,), True))

        def first_steps(step, carry):
            each(lambda c: visit(step, c, (0,), True))

            @pl.when(step == 1)
            def _():
                settle_own(0)

            @pl.when(step > 1)
            def _():
                settle(step - 1, (0,))

            return carry

        lax.fori_loop(1, early + 1, first_steps, 0)
        exchange.wait()
        each(lambda c: unit(at, c, (1,), True))
        lax.fori_loop(1, early + 1, lambda t, carry: (each(lambda c: visit(t, c, (1,), False)), carry)[1], 0)
        settle(early, (0,))

        def late_step(step, carry):
            each(lambda c: visit(step, c, (0, 1), True))

            @pl.when(step == early + 1)
            def _():
                settle_own(1)
                lax.fori_loop(1, early + 1, lambda t, inner: (settle(t, (1,)), inner)[1], 0)

            @pl.when(step > early + 1)
            def _():
                settle(step - 1, (0, 1))

            return carry

        if line - 1 > early:
            lax.fori_loop(early + 1, line, late_step, 0)
            settle(line - 1, (0, 1))
        else:
            settle_own(1)
            lax.fori_loop(1, early + 1, lambda t, inner: (settle(t, (1,)), inner)[1], 0)

        for way in range(2):
            for step in range(2):

                def finish(c):
                    @pl.when(leaves(way, step))
                    def _():
                        copy(way, step, c, step == 0).wait_send()

                if step == 0:
                    each(finish)
                else:

                    def finish_rest(t, carry):
                        def one(c):
                            @pl.when(leaves(way, t))
                            def _():
                                copy(way, t, c, False).wait_send()

                        each(one)
                        return carry

                    lax.fori_loop(1, line, finish_rest, 0)

        def drain(i, carry):
            for j in range(2):
                for k in range(1, heads):
                    to_head(i, j, mine, lax.rem(mine + k, heads)).wait_send()

                @pl.when(i != at)
                def _():
                    to_row(i, j, at).wait_send()
                    to_row(at, j, i).wait_recv()

            return carry

        lax.fori_loop(0, line, drain, 0)
        for i in range(n):
            out_ref[:, i * columns : (i + 1) * columns] = landed[i]

    return start_own, each, run


def project_kernel(n, heads, *refs):
    start_own, each, run = project_stages(n, heads, *refs)
    each(start_own)
    run()


def join_kernel(n, heads, o_ref, lse_ref, w_hbm, out_ref, x_ref, *refs):
    start_own, _, run = project_stages(n, heads, x_ref, w_hbm, out_ref, *refs[8:])
    per_way = BLK * heads // x_ref.shape[0]

    def ready(way):
        for c in range(per_way):
            start_own(way * per_way + c)

    drain = reduce_kernel(n, True, o_ref, lse_ref, x_ref, *refs[:8], ready=ready)
    run()
    drain()


def project_plan(n, heads, rows, width, columns, dtype):
    share = rows // heads
    line = n // 2
    dma = pltpu.SemaphoreType.DMA
    scratch = [
        pltpu.VMEM((2, width, columns), dtype),
        pltpu.VMEM((line, rows, width), dtype),
        pltpu.VMEM((line, 2, heads, share, columns), dtype),
        pltpu.VMEM((line, 2, heads, share, columns), dtype),
        pltpu.VMEM((line, 2, share, columns), dtype),
        pltpu.VMEM((n, share, columns), dtype),
        dma((1,)),
        dma((1,)),
        dma((1,)),
        dma((2, line, heads)),
        dma((2, line, heads)),
        dma((line, 2, heads)),
        dma((line, 2, heads)),
        dma((line, 2)),
        dma((line, 2)),
    ]
    padded = max(columns, BLK)
    held = [
        ((2, width, padded), dtype),
        ((line + 2, rows, width), dtype),
        ((2, n, heads, share, padded), dtype),
        ((3, n, share, padded), dtype),
    ]
    return scratch, held


def reduce_plan(n, small, kv_here, group_width):
    dma = pltpu.SemaphoreType.DMA((2, n - 1, kv_here))
    scratch = [
        pltpu.VMEM((2, n - 1, kv_here, BLK, group_width), jnp.bfloat16),
        pltpu.VMEM((2, n - 1, kv_here, STAT, BLK), jnp.float32),
        pltpu.VMEM((2, 2, 1 if small else kv_here, BLK, group_width), jnp.bfloat16),
        pltpu.SemaphoreType.DMA((2, 2)),
        dma,
        dma,
        dma,
        dma,
    ]
    held = [
        ((2, n + 1, kv_here, BLK, group_width), jnp.bfloat16),
        ((2, 2 * n - 1, kv_here, STAT, BLK), jnp.float32),
    ]
    return scratch, held


def mixed_from(parts, lse, weight, n, heads, rows, width, small):
    _, kv_here, _, group_width = parts.shape
    columns = weight.shape[1]
    vmem = pl.BlockSpec(memory_space=pltpu.VMEM)
    anywhere = pl.BlockSpec(memory_space=pl.ANY)
    reduce_scratch, reduce_held = reduce_plan(n, small, kv_here, group_width)
    project_scratch, project_held = project_plan(n, heads, rows, width, columns, parts.dtype)
    attended = jax.ShapeDtypeStruct((rows, width), parts.dtype)
    out = jax.ShapeDtypeStruct((rows // heads, n * columns), parts.dtype)

    def call(kernel, number, in_specs, out_shape, scratch, held):
        return pl.pallas_call(
            kernel,
            in_specs=in_specs,
            out_specs=vmem,
            out_shape=out_shape,
            scratch_shapes=scratch,
            compiler_params=pltpu.CompilerParams(
                collective_id=number, has_side_effects=True, vmem_limit_bytes=grant(*held)
            ),
            cost_estimate=long_cost(),
        )

    if small:
        scratch = [pltpu.VMEM((rows, width), parts.dtype)] + reduce_scratch + project_scratch
        held = reduce_held + project_held + [(parts.shape, parts.dtype)]
        kernel = functools.partial(join_kernel, n, heads)
        return call(kernel, 1, [vmem, vmem, anywhere], out, scratch, held)(parts, lse, weight)

    def kernel(*refs):
        reduce_kernel(n, small, *refs)

    x = call(kernel, 1, [anywhere, vmem], attended, reduce_scratch, reduce_held)(parts, lse)
    kernel = functools.partial(project_kernel, n, heads)
    return call(kernel, 2, [vmem, anywhere], out, project_scratch, project_held)(x, weight)


def body(
    queries,
    self_keys,
    self_values,
    store_keys,
    store_values,
    kv_slot,
    neighbours,
    counts,
    out_weight,
):
    n = lax.axis_size("seq")
    head_count = lax.axis_size("head")
    local_blocks, degree = neighbours.shape
    local_rows, width = queries.shape
    store_blocks = store_keys.shape[0] // BLK
    all_blocks = local_blocks * n
    kv_here = store_keys.shape[1] // DH
    group_width = (H // KVH) * DH
    rows = (H // KVH) * BLK
    small = queries.size * n * queries.dtype.itemsize <= 8 << 20
    count_row = counts.reshape(1, local_blocks)
    stores = (self_keys, self_values, store_keys, store_values)
    cut = tuple(a.reshape(store_blocks, BLK, -1) for a in stores[2:])
    smem = pl.BlockSpec(memory_space=pltpu.SMEM)
    vmem = pl.BlockSpec(memory_space=pltpu.VMEM)
    params = pltpu.CompilerParams(vmem_limit_bytes=28 << 20)
    cost = pl.CostEstimate(flops=2_000_000_000, bytes_accessed=12 << 20, transcendentals=4_000_000)
    scratch = [
        pltpu.SMEM((degree + 1,), jnp.int32),
        pltpu.VMEM((kv_here, DH, rows), jnp.float32),
        pltpu.VMEM((kv_here, rows), jnp.float32),
        pltpu.VMEM((kv_here, rows), jnp.float32),
    ]
    part_shape = (all_blocks, kv_here, BLK, group_width)
    lse_shape = (all_blocks, kv_here, STAT, BLK)
    if small:
        all_queries, near, count, parts, lse = gathered(queries, neighbours, count_row, n, (kv_slot,) + stores[:2] + cut)
        parts, lse = pl.pallas_call(
            functools.partial(rest_kernel, local_blocks, store_blocks),
            in_specs=[smem] * 3 + [vmem] * 7,
            out_specs=[vmem, vmem],
            out_shape=[pltpu.VMEM(part_shape, jnp.bfloat16), pltpu.VMEM(lse_shape, jnp.float32)],
            scratch_shapes=scratch,
            input_output_aliases={8: 0, 9: 1},
            compiler_params=params,
            cost_estimate=cost,
        )(kv_slot, near, count, all_queries, *stores, parts, lse)
    else:
        all_queries, near, count = gathered(queries, neighbours, count_row, n, ())
        parts, lse = pl.pallas_call(
            functools.partial(part_kernel, local_blocks, store_blocks),
            grid=(all_blocks,),
            in_specs=[smem] * 3 + [pl.BlockSpec((BLK, width), lambda i: (i, 0))] + [vmem] * 4,
            out_specs=[
                pl.BlockSpec((1, kv_here, BLK, group_width), lambda i: (i, 0, 0, 0)),
                pl.BlockSpec((1, kv_here, STAT, BLK), lambda i: (i, 0, 0, 0)),
            ],
            out_shape=[
                jax.ShapeDtypeStruct(part_shape, jnp.bfloat16),
                jax.ShapeDtypeStruct(lse_shape, jnp.float32),
            ],
            scratch_shapes=scratch,
            compiler_params=params,
            cost_estimate=cost,
        )(kv_slot, near, count, all_queries, *stores)
    return mixed_from(parts, lse, out_weight, n, head_count, local_rows, width, small)


def solution(mesh):
    placed = (
        P("seq", "head"),
        P("seq", "head"),
        P("seq", "head"),
        P("seq", "head"),
        P("seq", "head"),
        P(),
        P("seq", None),
        P("seq"),
        P("head", "seq"),
    )
    return jax.shard_map(
        body, mesh=mesh, in_specs=placed, out_specs=P(("seq", "head"), None), check_vma=False
    )
```

profile of v0, /device:TPU:3, one launch (start us, length us, event | category | flops | bytes accessed | tf_op | source)
XLA Modules:
  0.0 151.2 jit_solution(1527192897451188074)
XLA Ops:
  0.0 0.0 copy-start
  0.0 0.0 copy-start.1
  0.0 0.0 copy-start.2
  0.0 0.0 copy-start.3
  0.0 0.0 copy-start.4
  0.0 51.2 %shard_map.91 = (bf16[2048,1024]{1,0:T(8,128)(2,1)S(1)}, s32[8,2,64]{2,1,0:T(2,128)S(1)}, s32[8,1,2]{2,1,0:T(1,128)S(1)}, bf16[16,2,128,512]{3,2,1,0:T(8,128)(2,1)S(1)}, f32[16,2,8,128]{3,2,1,0:T(8,128)S(1)}) custom-call(bf16[256,1024]{1,0:T(8,128)(2,1)} %refs_0_.2, s32[2,64]{1,0:T(2,128)} %refs_1_.1, s32[1,2]{1,0:T(1,128)} %bitcast.5, s32[256]{0:T(256)} %refs_0_.3, ...), custom_call_target="tpu_custom_call" | custom-call | flops 199999995904 | bytes 1048576 | tf_op jit(solution)/shard_map/pallas_call | solution.py:404
  51.3 0.0 copy-done
  51.3 0.0 copy-done.1
  51.3 0.0 copy-done.2
  51.3 0.0 copy-done.3
  51.3 0.0 copy-done.4
  51.3 0.0 copy-start.5
  51.3 5.3 %shard_map.92 = (bf16[16,2,128,512]{3,2,1,0:T(8,128)(2,1)S(1)}, f32[16,2,8,128]{3,2,1,0:T(8,128)S(1)}) custom-call(s32[256]{0:T(256)S(1)} %copy-done.4, s32[8,2,64]{2,1,0:T(2,128)S(1)} %get-tuple-element.12.refs_1_, s32[8,1,2]{2,1,0:T(1,128)S(1)} %get-tuple-element.13.refs_2_, ...), custom_call_target="tpu_custom_call", output_to_operand_aliasing={{0}: (8, {}), {1}: (9, {})} | custom-call | flops 2000000000 | bytes 12582912 | tf_op jit(solution)/shard_map/pallas_call | solution.py:933
  56.6 0.0 copy-done.5
  56.6 93.8 %shard_map.93 = bf16[64,4096]{1,0:T(8,128)(2,1)S(1)} custom-call(bf16[16,2,128,512]{3,2,1,0:T(8,128)(2,1)S(1)} %get-tuple-element.17.o_ref, f32[16,2,8,128]{3,2,1,0:T(8,128)S(1)} %get-tuple-element.18.lse_ref, bf16[1024,512]{1,0:T(8,128)(2,1)S(1)} %copy-done.5), custom_call_target="tpu_custom_call" | custom-call | flops 199999995904 | bytes 1048576 | tf_op jit(solution)/shard_map/pallas_call | solution.py:885
  150.4 0.8 copy.15
Async XLA Ops:
  0.0 51.3 %copy-start = (bf16[4096,256]{1,0:T(8,128)(2,1)S(1)}, bf16[4096,256]{1,0:T(8,128)(2,1)}, u32[]{:S(2)}) copy-start(bf16[4096,256]{1,0:T(8,128)(2,1)} %refs_6_.1) | copy-start | bytes 6291460
  0.0 51.3 %copy-start.1 = (bf16[4096,256]{1,0:T(8,128)(2,1)S(1)}, bf16[4096,256]{1,0:T(8,128)(2,1)}, u32[]{:S(2)}) copy-start(bf16[4096,256]{1,0:T(8,128)(2,1)} %refs_7_.1) | copy-start | bytes 6291460
  0.0 51.3 %copy-start.2 = (bf16[256,256]{1,0:T(8,128)(2,1)S(1)}, bf16[256,256]{1,0:T(8,128)(2,1)}, u32[]{:S(2)}) copy-start(bf16[256,256]{1,0:T(8,128)(2,1)} %refs_4_.3) | copy-start | bytes 393220
  0.0 51.3 %copy-start.3 = (bf16[256,256]{1,0:T(8,128)(2,1)S(1)}, bf16[256,256]{1,0:T(8,128)(2,1)}, u32[]{:S(2)}) copy-start(bf16[256,256]{1,0:T(8,128)(2,1)} %refs_5_.3) | copy-start | bytes 393220
  0.0 51.3 %copy-start.4 = (s32[256]{0:T(256)S(1)}, s32[256]{0:T(256)}, u32[]{:S(2)}) copy-start(s32[256]{0:T(256)} %refs_0_.3) | copy-start | bytes 3076
  51.3 5.3 %copy-start.5 = (bf16[1024,512]{1,0:T(8,128)(2,1)S(1)}, bf16[1024,512]{1,0:T(8,128)(2,1)}, u32[]{:S(2)}) copy-start(bf16[1024,512]{1,0:T(8,128)(2,1)} %w_hbm.1) | copy-start | bytes 3145732
where the time goes:
time: 153 us; the launch traced here: 151 us
  Pallas kernels  150 us (98%)
    pallas_call x1, Pallas kernels, mixed_from(): call(kernel, 1, [vmem, vmem, anywhere], out, scratch, held)  93.8 us
    pallas_call x1, Pallas kernels, gathered(): pl.pallas_call(functools.partial(gather_kernel, n, pieces, bool(early)),...  51.2 us
    pallas_call x1, Pallas kernels, body(): pl.pallas_call(functools.partial(rest_kernel, local_blocks, store_blocks)...  5.29 us

commit v1 on v0

--- a/solution.py
+++ b/solution.py
@@ -14,6 +14,7 @@
 NEG = -1e30
 STAT = 8
 SCAN = 4
+CUTS = 2
 LOG2E = 1.4426950408889634
 MESH = pl.DeviceIdType.MESH
 
@@ -262,12 +263,6 @@
     def piece_of(way, spot):
         return spot if way == 0 else pieces - 1 - spot
 
-    started = []
-    for spot in range(pieces):
-        for way in range(2):
-            one = copy(way, 0, piece_of(way, spot))
-            one.start()
-            started.append(one)
     table_copies = []
     for t, target in enumerate((nears_ref, counts_ref)):
         for k in range(1, n):
@@ -283,6 +278,12 @@
             )
     for one in table_copies:
         one.start()
+    started = []
+    for spot in range(pieces):
+        for way in range(2):
+            one = copy(way, 0, piece_of(way, spot))
+            one.start()
+            started.append(one)
 
     def first_listed(owner, inner):
         degree = near_ref.shape[1]
@@ -299,9 +300,8 @@
 
         return lax.fori_loop(0, degree // SCAN, look, jnp.int32(-1))
 
-    def row_work(owner, inner, mine):
+    def row_work(owner, inner, spot, mine):
         per_group = H // KVH
-        spot = first_listed(owner, inner)
         taken = jnp.maximum(spot, 0)
         missing = jnp.minimum(spot, 0).astype(jnp.float32) * -NEG
         first_row = pl.multiple_of(owner * rows + inner * BLK, BLK)
@@ -325,18 +325,18 @@
                 lse = lse + missing
             write_part(o_ref, lse_ref, owner * pieces + inner, g, weighed(values, p), total, lse)
 
-    def arrived(step, spot):
-        if not early:
-            return
-
-        def one(way, carry):
-            owner = ring_index(place - (1 - 2 * way) * step, n)
-            row_work(owner, spot + way * (pieces - 1 - 2 * spot), False)
-            return carry
-
-        lax.fori_loop(0, 2, one, 0)
-
-    if early:
+    def row_at(way, step, spot):
+        return ring_index(place - ways[way] * step, n), piece_of(way, spot)
+
+    def scanned(step, spot):
+        return [first_listed(*row_at(way, step, spot)) for way in range(2)] if early else None
+
+    def arrived(step, spot, found):
+        if early:
+            for way in range(2):
+                row_work(*row_at(way, step, spot), found[way], False)
+
+    def own_rows():
         for one in table_copies:
             one.wait_recv()
         tables = [
@@ -347,20 +347,28 @@
             one.start()
         for one in loads + tables:
             one.wait()
-        lax.fori_loop(0, pieces, lambda inner, carry: (row_work(me, inner, True), carry)[1], 0)
+        for inner in range(pieces):
+            row_work(me, inner, first_listed(me, inner), True)
+
     for step in range(1, half):
         for spot in range(pieces):
+            first = step == 1 and spot == 0
+            found = None if first else scanned(step, spot)
             for way in range(2):
                 copy(way, step - 1, piece_of(way, spot)).wait_recv()
                 if step < half - 1 or spot < pieces // 2:
                     one = copy(way, step, piece_of(way, spot))
                     one.start()
                     started.append(one)
-            arrived(step, spot)
+            if early and first:
+                own_rows()
+                found = scanned(step, spot)
+            arrived(step, spot, found)
     for spot in range(pieces // 2):
+        found = scanned(half, spot)
         for way in range(2):
             copy(way, half - 1, piece_of(way, spot)).wait_recv()
-        arrived(half, spot)
+        arrived(half, spot, found)
     for one in started:
         one.wait_send()
     for one in table_copies:
@@ -443,6 +451,7 @@
     me = lax.axis_index("seq")
     place = ring_place(me, n)
     groups, width = got.shape[2], got.shape[4]
+    wide = width // CUTS
     ways = (1, -1)
     beside = [ring_index(place + way, n) for way in ways]
     if ready is None:
@@ -458,44 +467,48 @@
             o_ref.at[home(way, step) * 2 + way], own.at[way, lax.rem(step, 2)], own_sem.at[way, lax.rem(step, 2)]
         )
 
-    def copies(way, step, g, before):
-        at = home(way, step) * 2 + way
-        first = before is None
-        return (
-            pltpu.make_async_remote_copy(
-                src_ref=lse_ref.at[at, g] if first else got_lse.at[way, before, g],
-                dst_ref=got_lse.at[way, step, g],
-                send_sem=lsend_sem.at[way, step, g],
-                recv_sem=lrecv_sem.at[way, step, g],
-                device_id={"seq": beside[way]},
-                device_id_type=MESH,
-            ),
-            pltpu.make_async_remote_copy(
-                src_ref=o_ref.at[at, g] if first else got.at[way, before, g],
-                dst_ref=got.at[way, step, g],
-                send_sem=send_sem.at[way, step, g],
-                recv_sem=recv_sem.at[way, step, g],
-                device_id={"seq": beside[way]},
-                device_id_type=MESH,
-            ),
+    def lse_copy(way, step, g, before):
+        return pltpu.make_async_remote_copy(
+            src_ref=lse_ref.at[home(way, step) * 2 + way, g] if before is None else got_lse.at[way, before, g],
+            dst_ref=got_lse.at[way, step, g],
+            send_sem=lsend_sem.at[way, step, g],
+            recv_sem=lrecv_sem.at[way, step, g],
+            device_id={"seq": beside[way]},
+            device_id_type=MESH,
         )
 
-    def merged(way, step, g):
-        for one in copies(way, step - 1, g, step - 1):
-            one.wait_recv()
+    def copy(way, step, g, cut, before):
+        part = (g, slice(None), pl.ds(cut * wide, wide))
+        return pltpu.make_async_remote_copy(
+            src_ref=o_ref.at[(home(way, step) * 2 + way,) + part]
+            if before is None
+            else got.at[(way, before) + part],
+            dst_ref=got.at[(way, step) + part],
+            send_sem=send_sem.at[way, step, g * CUTS + cut],
+            recv_sem=recv_sem.at[way, step, g * CUTS + cut],
+            device_id={"seq": beside[way]},
+            device_id_type=MESH,
+        )
+
+    def shares_of(way, step, g):
+        lse_copy(way, step - 1, g, step - 1).wait_recv()
         if g == 0 and not small:
             fetch(way, step).wait()
+        return merge(got_lse[way, step - 1, g], lse_ref[home(way, step) * 2 + way, g])
+
+    def merged(way, step, g, cut, theirs, ours):
+        copy(way, step - 1, g, cut, step - 1).wait_recv()
         at = home(way, step) * 2 + way
-        theirs, ours, lse = merge(got_lse[way, step - 1, g], lse_ref[at, g])
         columns = []
-        for r in range(width // DH):
+        for r in range(cut * wide // DH, (cut + 1) * wide // DH):
             cols = slice(r * DH, (r + 1) * DH)
             mine = o_ref[at, g, :, cols] if small else own[way, lax.rem(step, 2), g, :, cols]
-            columns.append(
+            value = (
                 got[way, step - 1, g, :, cols].astype(jnp.float32) * theirs[r : r + 1]
                 + mine.astype(jnp.float32) * ours[r : r + 1]
             )
-        return columns, lse
+            columns.append((r, value))
+        return columns
 
     if not small:
         for way in range(2):
@@ -504,47 +517,50 @@
         pl.semaphore_wait(barrier, 2)
     for g in range(groups):
         for way in range(2):
-            for one in copies(way, 0, g, None):
-                one.start()
+            lse_copy(way, 0, g, None).start()
+        for cut in range(CUTS):
+            for way in range(2):
+                copy(way, 0, g, cut, None).start()
 
     def one_step(step, carry):
         if not small:
             for way in range(2):
                 fetch(way, step + 1).start()
         for g in range(groups):
+            shares = []
             for way in range(2):
-                columns, lse = merged(way, step, g)
+                theirs, ours, lse = shares_of(way, step, g)
                 got_lse[way, step - 1, g] = lse
-                for r, value in enumerate(columns):
-                    got[way, step - 1, g, :, r * DH : (r + 1) * DH] = value.astype(jnp.bfloat16)
-                for one in copies(way, step, g, step - 1):
-                    one.start()
+                lse_copy(way, step, g, step - 1).start()
+                shares.append((theirs, ours))
+            for cut in range(CUTS):
+                for way in range(2):
+                    for r, value in merged(way, step, g, cut, *shares[way]):
+                        got[way, step - 1, g, :, r * DH : (r + 1) * DH] = value.astype(jnp.bfloat16)
+                    copy(way, step, g, cut, step - 1).start()
         return carry
 
     lax.fori_loop(1, n - 1, one_step, 0)
     for way in range(2):
         for g in range(groups):
-            columns, _ = merged(way, n - 1, g)
-            for r, value in enumerate(columns):
-                at = g * width + r * DH
-                out_ref[way * BLK : (way + 1) * BLK, at : at + DH] = jnp.transpose(value).astype(jnp.bfloat16)
+            theirs, ours, _ = shares_of(way, n - 1, g)
+            for cut in range(CUTS):
+                for r, value in merged(way, n - 1, g, cut, theirs, ours):
+                    at = g * width + r * DH
+                    out_ref[way * BLK : (way + 1) * BLK, at : at + DH] = jnp.transpose(value).astype(jnp.bfloat16)
         if ready is not None:
             ready(way)
 
     def drain_all():
-        for g in range(groups):
-            for way in range(2):
-                for one in copies(way, 0, g, None):
-                    one.wait_send()
-
-        def drain(step, carry):
+        def drain(step, before):
             for g in range(groups):
                 for way in range(2):
-                    for one in copies(way, step, g, step - 1):
-                        one.wait_send()
-            return carry
-
-        lax.fori_loop(1, n - 1, drain, 0)
+                    lse_copy(way, step, g, before).wait_send()
+                    for cut in range(CUTS):
+                        copy(way, step, g, cut, before).wait_send()
+
+        drain(0, None)
+        lax.fori_loop(1, n - 1, lambda step, carry: (drain(step, step - 1), carry)[1], 0)
 
     if ready is None:
         drain_all()
@@ -838,13 +854,14 @@
 
 def reduce_plan(n, small, kv_here, group_width):
     dma = pltpu.SemaphoreType.DMA((2, n - 1, kv_here))
+    dma_cuts = pltpu.SemaphoreType.DMA((2, n - 1, kv_here * CUTS))
     scratch = [
         pltpu.VMEM((2, n - 1, kv_here, BLK, group_width), jnp.bfloat16),
         pltpu.VMEM((2, n - 1, kv_here, STAT, BLK), jnp.float32),
         pltpu.VMEM((2, 2, 1 if small else kv_here, BLK, group_width), jnp.bfloat16),
         pltpu.SemaphoreType.DMA((2, 2)),
-        dma,
-        dma,
+        dma_cuts,
+        dma_cuts,
         dma,
         dma,
     ]

time: 153 us -> 149 us (0.974)
  Pallas kernels: 150 us -> 146 us
    pallas_call x1, Pallas kernels: 51.2 us -> 46.2 us  [gathered(): pl.pallas_call(functools.partial(gather_kernel, n, pieces, bool(early)),...]
where the time goes in v1:
time: 149 us; the launch traced here: 147 us
  Pallas kernels  146 us (98%)
    pallas_call x1, Pallas kernels, mixed_from(): call(kernel, 1, [vmem, vmem, anywhere], out, scratch, held)  94.6 us
    pallas_call x1, Pallas kernels, gathered(): pl.pallas_call(functools.partial(gather_kernel, n, pieces, bool(early)),...  46.2 us
    pallas_call x1, Pallas kernels, body(): pl.pallas_call(functools.partial(rest_kernel, local_blocks, store_blocks)...  5.26 us

profile of v1, /device:TPU:3, one launch (start us, length us, event | category | flops | bytes accessed | tf_op | source)
XLA Modules:
  0.0 147.0 jit_solution(7421308432641197248)
XLA Ops:
  0.0 0.0 copy-start
  0.0 0.0 copy-start.1
  0.0 0.0 copy-start.2
  0.0 0.0 copy-start.3
  0.0 0.0 copy-start.4
  0.0 46.2 %shard_map.91 = (bf16[2048,1024]{1,0:T(8,128)(2,1)S(1)}, s32[8,2,64]{2,1,0:T(2,128)S(1)}, s32[8,1,2]{2,1,0:T(1,128)S(1)}, bf16[16,2,128,512]{3,2,1,0:T(8,128)(2,1)S(1)}, f32[16,2,8,128]{3,2,1,0:T(8,128)S(1)}) custom-call(bf16[256,1024]{1,0:T(8,128)(2,1)} %refs_0_.2, s32[2,64]{1,0:T(2,128)} %refs_1_.1, s32[1,2]{1,0:T(1,128)} %bitcast.5, s32[256]{0:T(256)} %refs_0_.3, ...), custom_call_target="tpu_custom_call" | custom-call | flops 199999995904 | bytes 1048576 | tf_op jit(solution)/shard_map/pallas_call | solution.py:412
  46.2 0.0 copy-done
  46.3 0.0 copy-done.1
  46.3 0.0 copy-done.2
  46.3 0.0 copy-done.3
  46.3 0.0 copy-done.4
  46.3 0.0 copy-start.5
  46.3 5.3 %shard_map.92 = (bf16[16,2,128,512]{3,2,1,0:T(8,128)(2,1)S(1)}, f32[16,2,8,128]{3,2,1,0:T(8,128)S(1)}) custom-call(s32[256]{0:T(256)S(1)} %copy-done.4, s32[8,2,64]{2,1,0:T(2,128)S(1)} %get-tuple-element.12.refs_1_, s32[8,1,2]{2,1,0:T(1,128)S(1)} %get-tuple-element.13.refs_2_, ...), custom_call_target="tpu_custom_call", output_to_operand_aliasing={{0}: (8, {}), {1}: (9, {})} | custom-call | flops 2000000000 | bytes 12582912 | tf_op jit(solution)/shard_map/pallas_call | solution.py:950
  51.6 0.0 copy-done.5
  51.6 94.6 %shard_map.93 = bf16[64,4096]{1,0:T(8,128)(2,1)S(1)} custom-call(bf16[16,2,128,512]{3,2,1,0:T(8,128)(2,1)S(1)} %get-tuple-element.17.o_ref, f32[16,2,8,128]{3,2,1,0:T(8,128)S(1)} %get-tuple-element.18.lse_ref, bf16[1024,512]{1,0:T(8,128)(2,1)S(1)} %copy-done.5), custom_call_target="tpu_custom_call" | custom-call | flops 199999995904 | bytes 1048576 | tf_op jit(solution)/shard_map/pallas_call | solution.py:902
  146.2 0.8 copy.15
Async XLA Ops:
  0.0 46.2 %copy-start = (bf16[4096,256]{1,0:T(8,128)(2,1)S(1)}, bf16[4096,256]{1,0:T(8,128)(2,1)}, u32[]{:S(2)}) copy-start(bf16[4096,256]{1,0:T(8,128)(2,1)} %refs_6_.1) | copy-start | bytes 6291460
  0.0 46.3 %copy-start.1 = (bf16[4096,256]{1,0:T(8,128)(2,1)S(1)}, bf16[4096,256]{1,0:T(8,128)(2,1)}, u32[]{:S(2)}) copy-start(bf16[4096,256]{1,0:T(8,128)(2,1)} %refs_7_.1) | copy-start | bytes 6291460
  0.0 46.3 %copy-start.2 = (bf16[256,256]{1,0:T(8,128)(2,1)S(1)}, bf16[256,256]{1,0:T(8,128)(2,1)}, u32[]{:S(2)}) copy-start(bf16[256,256]{1,0:T(8,128)(2,1)} %refs_4_.3) | copy-start | bytes 393220
  0.0 46.3 %copy-start.3 = (bf16[256,256]{1,0:T(8,128)(2,1)S(1)}, bf16[256,256]{1,0:T(8,128)(2,1)}, u32[]{:S(2)}) copy-start(bf16[256,256]{1,0:T(8,128)(2,1)} %refs_5_.3) | copy-start | bytes 393220
  0.0 46.3 %copy-start.4 = (s32[256]{0:T(256)S(1)}, s32[256]{0:T(256)}, u32[]{:S(2)}) copy-start(s32[256]{0:T(256)} %refs_0_.3) | copy-start | bytes 3076
  46.3 5.3 %copy-start.5 = (bf16[1024,512]{1,0:T(8,128)(2,1)S(1)}, bf16[1024,512]{1,0:T(8,128)(2,1)}, u32[]{:S(2)}) copy-start(bf16[1024,512]{1,0:T(8,128)(2,1)} %w_hbm.1) | copy-start | bytes 3145732

commit v2 on v1

--- a/solution.py
+++ b/solution.py
@@ -570,6 +570,7 @@
 def project_stages(
     n,
     heads,
+    joined,
     x_ref,
     w_hbm,
     out_ref,
@@ -606,12 +607,13 @@
         pl.semaphore_signal(barrier, inc=1, device_id={"seq": other}, device_id_type=MESH)
     for k in range(1, heads):
         pl.semaphore_signal(barrier, inc=1, device_id={"head": lax.rem(mine + k, heads)}, device_id_type=MESH)
-    for k in range(1, line):
-        other = lax.rem(at + k, line) * 2 + side
-        pl.semaphore_signal(barrier, inc=1, device_id={"seq": other}, device_id_type=MESH)
     partner = at * 2 + 1 - side
-    pl.semaphore_signal(barrier, inc=1, device_id={"seq": partner}, device_id_type=MESH)
-    pl.semaphore_wait(barrier, heads + line + 1)
+    if not joined:
+        for k in range(1, line):
+            other = lax.rem(at + k, line) * 2 + side
+            pl.semaphore_signal(barrier, inc=1, device_id={"seq": other}, device_id_type=MESH)
+        pl.semaphore_signal(barrier, inc=1, device_id={"seq": partner}, device_id_type=MESH)
+    pl.semaphore_wait(barrier, heads + 1 if joined else heads + line + 1)
 
     def inside(spot):
         return jnp.logical_and(spot >= 0, spot < line)
@@ -739,26 +741,38 @@
         lax.fori_loop(1, early + 1, lambda t, carry: (each(lambda c: visit(t, c, (1,), False)), carry)[1], 0)
         settle(early, (0,))
 
+        def settle_early():
+            settle_own(1)
+            lax.fori_loop(1, early + 1, lambda t, carry: (settle(t, (1,)), carry)[1], 0)
+
         def late_step(step, carry):
-            each(lambda c: visit(step, c, (0, 1), True))
-
-            @pl.when(step == early + 1)
-            def _():
-                settle_own(1)
-                lax.fori_loop(1, early + 1, lambda t, inner: (settle(t, (1,)), inner)[1], 0)
-
-            @pl.when(step > early + 1)
-            def _():
-                settle(step - 1, (0, 1))
-
+            def late_visit(c):
+                visit(step, c, (0, 1), True)
+
+                @pl.when(jnp.logical_and(c == 0, step == early + 1))
+                def _():
+                    settle_early()
+
+                @pl.when(jnp.logical_and(c == 0, step > early + 1))
+                def _():
+                    settle(step - 1, (0, 1))
+
+                @pl.when(jnp.logical_and(mine == c - 1, step == line - 1))
+                def _():
+                    settle(step, (0, 1))
+
+            each(late_visit)
             return carry
 
         if line - 1 > early:
             lax.fori_loop(early + 1, line, late_step, 0)
-            settle(line - 1, (0, 1))
+
+            @pl.when(mine == heads - 1)
+            def _():
+                settle(line - 1, (0, 1))
+
         else:
-            settle_own(1)
-            lax.fori_loop(1, early + 1, lambda t, inner: (settle(t, (1,)), inner)[1], 0)
+            settle_early()
 
         for way in range(2):
             for step in range(2):
@@ -803,13 +817,13 @@
 
 
 def project_kernel(n, heads, *refs):
-    start_own, each, run = project_stages(n, heads, *refs)
+    start_own, each, run = project_stages(n, heads, False, *refs)
     each(start_own)
     run()
 
 
 def join_kernel(n, heads, o_ref, lse_ref, w_hbm, out_ref, x_ref, *refs):
-    start_own, _, run = project_stages(n, heads, x_ref, w_hbm, out_ref, *refs[8:])
+    start_own, _, run = project_stages(n, heads, True, x_ref, w_hbm, out_ref, *refs[8:])
     per_way = BLK * heads // x_ref.shape[0]
 
     def ready(way):

time: 149 us -> 149 us (level)
  no operation moved by 1% of the time
where the time goes in v2:
time: 149 us; the launch traced here: 148 us
  Pallas kernels  147 us (99%)
    pallas_call x1, Pallas kernels, mixed_from(): call(kernel, 1, [vmem, vmem, anywhere], out, scratch, held)  95.1 us
    pallas_call x1, Pallas kernels, gathered(): pl.pallas_call(functools.partial(gather_kernel, n, pieces, bool(early)),...  46.2 us
    pallas_call x1, Pallas kernels, body(): pl.pallas_call(functools.partial(rest_kernel, local_blocks, store_blocks)...  6.01 us

profile of v2, /device:TPU:3, one launch (start us, length us, event | category | flops | bytes accessed | tf_op | source)
XLA Modules:
  0.0 148.3 jit_solution(11413028576642993101)
XLA Ops:
  0.0 0.0 copy-start
  0.0 0.0 copy-start.1
  0.0 0.0 copy-start.2
  0.0 0.0 copy-start.3
  0.0 0.0 copy-start.4
  0.0 46.2 %shard_map.91 = (bf16[2048,1024]{1,0:T(8,128)(2,1)S(1)}, s32[8,2,64]{2,1,0:T(2,128)S(1)}, s32[8,1,2]{2,1,0:T(1,128)S(1)}, bf16[16,2,128,512]{3,2,1,0:T(8,128)(2,1)S(1)}, f32[16,2,8,128]{3,2,1,0:T(8,128)S(1)}) custom-call(bf16[256,1024]{1,0:T(8,128)(2,1)} %refs_0_.2, s32[2,64]{1,0:T(2,128)} %refs_1_.1, s32[1,2]{1,0:T(1,128)} %bitcast.5, s32[256]{0:T(256)} %refs_0_.3, ...), custom_call_target="tpu_custom_call" | custom-call | flops 199999995904 | bytes 1048576 | tf_op jit(solution)/shard_map/pallas_call | solution.py:412
  46.2 0.0 copy-done
  46.3 0.0 copy-done.1
  46.3 0.0 copy-done.2
  46.3 0.0 copy-done.3
  46.3 0.0 copy-done.4
  46.3 0.0 copy-start.5
  46.3 6.0 %shard_map.92 = (bf16[16,2,128,512]{3,2,1,0:T(8,128)(2,1)S(1)}, f32[16,2,8,128]{3,2,1,0:T(8,128)S(1)}) custom-call(s32[256]{0:T(256)S(1)} %copy-done.4, s32[8,2,64]{2,1,0:T(2,128)S(1)} %get-tuple-element.12.refs_1_, s32[8,1,2]{2,1,0:T(1,128)S(1)} %get-tuple-element.13.refs_2_, ...), custom_call_target="tpu_custom_call", output_to_operand_aliasing={{0}: (8, {}), {1}: (9, {})} | custom-call | flops 2000000000 | bytes 12582912 | tf_op jit(solution)/shard_map/pallas_call | solution.py:964
  52.3 0.0 copy-done.5
  52.3 95.1 %shard_map.93 = bf16[64,4096]{1,0:T(8,128)(2,1)S(1)} custom-call(bf16[16,2,128,512]{3,2,1,0:T(8,128)(2,1)S(1)} %get-tuple-element.17.o_ref, f32[16,2,8,128]{3,2,1,0:T(8,128)S(1)} %get-tuple-element.18.lse_ref, bf16[1024,512]{1,0:T(8,128)(2,1)S(1)} %copy-done.5), custom_call_target="tpu_custom_call" | custom-call | flops 199999995904 | bytes 1048576 | tf_op jit(solution)/shard_map/pallas_call | solution.py:916
  147.5 0.8 copy.15
Async XLA Ops:
  0.0 46.2 %copy-start = (bf16[4096,256]{1,0:T(8,128)(2,1)S(1)}, bf16[4096,256]{1,0:T(8,128)(2,1)}, u32[]{:S(2)}) copy-start(bf16[4096,256]{1,0:T(8,128)(2,1)} %refs_6_.1) | copy-start | bytes 6291460
  0.0 46.3 %copy-start.1 = (bf16[4096,256]{1,0:T(8,128)(2,1)S(1)}, bf16[4096,256]{1,0:T(8,128)(2,1)}, u32[]{:S(2)}) copy-start(bf16[4096,256]{1,0:T(8,128)(2,1)} %refs_7_.1) | copy-start | bytes 6291460
  0.0 46.3 %copy-start.2 = (bf16[256,256]{1,0:T(8,128)(2,1)S(1)}, bf16[256,256]{1,0:T(8,128)(2,1)}, u32[]{:S(2)}) copy-start(bf16[256,256]{1,0:T(8,128)(2,1)} %refs_4_.3) | copy-start | bytes 393220
  0.0 46.3 %copy-start.3 = (bf16[256,256]{1,0:T(8,128)(2,1)S(1)}, bf16[256,256]{1,0:T(8,128)(2,1)}, u32[]{:S(2)}) copy-start(bf16[256,256]{1,0:T(8,128)(2,1)} %refs_5_.3) | copy-start | bytes 393220
  0.0 46.3 %copy-start.4 = (s32[256]{0:T(256)S(1)}, s32[256]{0:T(256)}, u32[]{:S(2)}) copy-start(s32[256]{0:T(256)} %refs_0_.3) | copy-start | bytes 3076
  46.3 6.0 %copy-start.5 = (bf16[1024,512]{1,0:T(8,128)(2,1)S(1)}, bf16[1024,512]{1,0:T(8,128)(2,1)}, u32[]{:S(2)}) copy-start(bf16[1024,512]{1,0:T(8,128)(2,1)} %w_hbm.1) | copy-start | bytes 3145732

commit v3 on v2

--- a/solution.py
+++ b/solution.py
@@ -12,9 +12,8 @@
 DH = 128
 BLK = 128
 NEG = -1e30
-STAT = 8
 SCAN = 4
-CUTS = 2
+CUTS = 1
 LOG2E = 1.4426950408889634
 MESH = pl.DeviceIdType.MESH
 
@@ -48,9 +47,9 @@
 def write_part(o_ref, lse_ref, here, g, acc, total, lse):
     per_group = lse.shape[1] // BLK
     o_ref[here, g] = (acc * (1.0 / total)).astype(jnp.bfloat16)
-    for r in range(STAT):
-        at = (r % per_group) * BLK
-        lse_ref[here, g, r : r + 1] = lse[:, at : at + BLK]
+    for r in range(per_group):
+        head = g * per_group + r
+        lse_ref[here, head : head + 1] = lse[:, r * BLK : (r + 1) * BLK]
 
 
 def part_row(
@@ -105,7 +104,11 @@
         if done:
             for g in range(kv_here):
                 max_ref[g : g + 1] = jnp.concatenate(
-                    [lse_ref[here, g, r : r + 1] for r in range(per_group)], axis=1
+                    [
+                        lse_ref[here, head : head + 1]
+                        for head in range(g * per_group, (g + 1) * per_group)
+                    ],
+                    axis=1,
                 )
                 sum_ref[g : g + 1] = jnp.ones((1, rows), jnp.float32)
                 acc_ref[g] = o_ref[here, g].astype(jnp.float32)
@@ -396,7 +399,7 @@
         slot, *stores = early
         kv_here = stores[2].shape[2] // DH
         part_shape = (n * pieces, kv_here, BLK, (H // KVH) * DH)
-        out_shape += [kind(part_shape, x.dtype), kind((n * pieces, kv_here, STAT, BLK), jnp.float32)]
+        out_shape += [kind(part_shape, x.dtype), kind((n * pieces, kv_here * (H // KVH), BLK), jnp.float32)]
         scratch += [pltpu.SMEM(slot.shape, slot.dtype)]
         scratch += [pltpu.SMEM(out_shape[1].shape, near.dtype), pltpu.SMEM(out_shape[2].shape, count.dtype)]
         scratch += [pltpu.VMEM(a.shape, a.dtype) for a in stores]
@@ -467,12 +470,12 @@
             o_ref.at[home(way, step) * 2 + way], own.at[way, lax.rem(step, 2)], own_sem.at[way, lax.rem(step, 2)]
         )
 
-    def lse_copy(way, step, g, before):
+    def lse_copy(way, step, before):
         return pltpu.make_async_remote_copy(
-            src_ref=lse_ref.at[home(way, step) * 2 + way, g] if before is None else got_lse.at[way, before, g],
-            dst_ref=got_lse.at[way, step, g],
-            send_sem=lsend_sem.at[way, step, g],
-            recv_sem=lrecv_sem.at[way, step, g],
+            src_ref=lse_ref.at[home(way, step) * 2 + way] if before is None else got_lse.at[way, before],
+            dst_ref=got_lse.at[way, step],
+            send_sem=lsend_sem.at[way, step],
+            recv_sem=lrecv_sem.at[way, step],
             device_id={"seq": beside[way]},
             device_id_type=MESH,
         )
@@ -490,11 +493,11 @@
             device_id_type=MESH,
         )
 
-    def shares_of(way, step, g):
-        lse_copy(way, step - 1, g, step - 1).wait_recv()
-        if g == 0 and not small:
+    def shares_of(way, step):
+        lse_copy(way, step - 1, step - 1).wait_recv()
+        if not small:
             fetch(way, step).wait()
-        return merge(got_lse[way, step - 1, g], lse_ref[home(way, step) * 2 + way, g])
+        return merge(got_lse[way, step - 1], lse_ref[home(way, step) * 2 + way])
 
     def merged(way, step, g, cut, theirs, ours):
         copy(way, step - 1, g, cut, step - 1).wait_recv()
@@ -502,10 +505,11 @@
         columns = []
         for r in range(cut * wide // DH, (cut + 1) * wide // DH):
             cols = slice(r * DH, (r + 1) * DH)
+            head = g * (width // DH) + r
             mine = o_ref[at, g, :, cols] if small else own[way, lax.rem(step, 2), g, :, cols]
             value = (
-                got[way, step - 1, g, :, cols].astype(jnp.float32) * theirs[r : r + 1]
-                + mine.astype(jnp.float32) * ours[r : r + 1]
+                got[way, step - 1, g, :, cols].astype(jnp.float32) * theirs[head : head + 1]
+                + mine.astype(jnp.float32) * ours[head : head + 1]
             )
             columns.append((r, value))
         return columns
@@ -515,9 +519,9 @@
             fetch(way, 1).start()
     if ready is None:
         pl.semaphore_wait(barrier, 2)
+    for way in range(2):
+        lse_copy(way, 0, None).start()
     for g in range(groups):
-        for way in range(2):
-            lse_copy(way, 0, g, None).start()
         for cut in range(CUTS):
             for way in range(2):
                 copy(way, 0, g, cut, None).start()
@@ -526,13 +530,13 @@
         if not small:
             for way in range(2):
                 fetch(way, step + 1).start()
+        shares = []
+        for way in range(2):
+            theirs, ours, lse = shares_of(way, step)
+            got_lse[way, step - 1] = lse
+            lse_copy(way, step, step - 1).start()
+            shares.append((theirs, ours))
         for g in range(groups):
-            shares = []
-            for way in range(2):
-                theirs, ours, lse = shares_of(way, step, g)
-                got_lse[way, step - 1, g] = lse
-                lse_copy(way, step, g, step - 1).start()
-                shares.append((theirs, ours))
             for cut in range(CUTS):
                 for way in range(2):
                     for r, value in merged(way, step, g, cut, *shares[way]):
@@ -542,8 +546,8 @@
 
     lax.fori_loop(1, n - 1, one_step, 0)
     for way in range(2):
+        theirs, ours, _ = shares_of(way, n - 1)
         for g in range(groups):
-            theirs, ours, _ = shares_of(way, n - 1, g)
             for cut in range(CUTS):
                 for r, value in merged(way, n - 1, g, cut, theirs, ours):
                     at = g * width + r * DH
@@ -553,9 +557,9 @@
 
     def drain_all():
         def drain(step, before):
-            for g in range(groups):
-                for way in range(2):
-                    lse_copy(way, step, g, before).wait_send()
+            for way in range(2):
+                lse_copy(way, step, before).wait_send()
+                for g in range(groups):
                     for cut in range(CUTS):
                         copy(way, step, g, cut, before).wait_send()
 
@@ -867,11 +871,12 @@
 
 
 def reduce_plan(n, small, kv_here, group_width):
-    dma = pltpu.SemaphoreType.DMA((2, n - 1, kv_here))
+    heads_here = kv_here * (H // KVH)
+    dma = pltpu.SemaphoreType.DMA((2, n - 1))
     dma_cuts = pltpu.SemaphoreType.DMA((2, n - 1, kv_here * CUTS))
     scratch = [
         pltpu.VMEM((2, n - 1, kv_here, BLK, group_width), jnp.bfloat16),
-        pltpu.VMEM((2, n - 1, kv_here, STAT, BLK), jnp.float32),
+        pltpu.VMEM((2, n - 1, heads_here, BLK), jnp.float32),
         pltpu.VMEM((2, 2, 1 if small else kv_here, BLK, group_width), jnp.bfloat16),
         pltpu.SemaphoreType.DMA((2, 2)),
         dma_cuts,
@@ -881,7 +886,7 @@
     ]
     held = [
         ((2, n + 1, kv_here, BLK, group_width), jnp.bfloat16),
-        ((2, 2 * n - 1, kv_here, STAT, BLK), jnp.float32),
+        ((2, 2 * n - 1, heads_here, BLK), jnp.float32),
     ]
     return scratch, held
 
@@ -958,7 +963,7 @@
         pltpu.VMEM((kv_here, rows), jnp.float32),
     ]
     part_shape = (all_blocks, kv_here, BLK, group_width)
-    lse_shape = (all_blocks, kv_here, STAT, BLK)
+    lse_shape = (all_blocks, kv_here * (H // KVH), BLK)
     if small:
         all_queries, near, count, parts, lse = gathered(queries, neighbours, count_row, n, (kv_slot,) + stores[:2] + cut)
         parts, lse = pl.pallas_call(
@@ -979,7 +984,7 @@
             in_specs=[smem] * 3 + [pl.BlockSpec((BLK, width), lambda i: (i, 0))] + [vmem] * 4,
             out_specs=[
                 pl.BlockSpec((1, kv_here, BLK, group_width), lambda i: (i, 0, 0, 0)),
-                pl.BlockSpec((1, kv_here, STAT, BLK), lambda i: (i, 0, 0, 0)),
+                pl.BlockSpec((1, kv_here * (H // KVH), BLK), lambda i: (i, 0, 0)),
             ],
             out_shape=[
                 jax.ShapeDtypeStruct(part_shape, jnp.bfloat16),

time: 149 us -> 148 us (level)
  no operation moved by 1% of the time
where the time goes in v3:
time: 148 us; the launch traced here: 149 us
  Pallas kernels  148 us (100%)
    pallas_call x1, Pallas kernels, mixed_from(): call(kernel, 1, [vmem, vmem, anywhere], out, scratch, held)  96.3 us
    pallas_call x1, Pallas kernels, gathered(): pl.pallas_call(functools.partial(gather_kernel, n, pieces, bool(early)),...  46.2 us
    pallas_call x1, Pallas kernels, body(): pl.pallas_call(functools.partial(rest_kernel, local_blocks, store_blocks)...  5.29 us

profile of v3, /device:TPU:3, one launch (start us, length us, event | category | flops | bytes accessed | tf_op | source)
XLA Modules:
  0.0 148.7 jit_solution(14944017985941839053)
XLA Ops:
  0.0 0.0 copy-start
  0.0 0.0 copy-start.1
  0.0 0.0 copy-start.2
  0.0 0.0 copy-start.3
  0.0 0.0 copy-start.4
  0.0 46.2 %shard_map.91 = (bf16[2048,1024]{1,0:T(8,128)(2,1)S(1)}, s32[8,2,64]{2,1,0:T(2,128)S(1)}, s32[8,1,2]{2,1,0:T(1,128)S(1)}, bf16[16,2,128,512]{3,2,1,0:T(8,128)(2,1)S(1)}, f32[16,8,128]{2,1,0:T(8,128)S(1)}) custom-call(bf16[256,1024]{1,0:T(8,128)(2,1)} %refs_0_.2, s32[2,64]{1,0:T(2,128)} %refs_1_.1, s32[1,2]{1,0:T(1,128)} %bitcast.5, s32[256]{0:T(256)} %refs_0_.3, ...), custom_call_target="tpu_custom_call" | custom-call | flops 199999995904 | bytes 1048576 | tf_op jit(solution)/shard_map/pallas_call | solution.py:415
  46.2 0.0 copy-done
  46.3 0.0 copy-done.1
  46.3 0.0 copy-done.2
  46.3 0.0 copy-done.3
  46.3 0.0 copy-done.4
  46.3 0.0 copy-start.5
  46.3 5.3 %shard_map.92 = (bf16[16,2,128,512]{3,2,1,0:T(8,128)(2,1)S(1)}, f32[16,8,128]{2,1,0:T(8,128)S(1)}) custom-call(s32[256]{0:T(256)S(1)} %copy-done.4, s32[8,2,64]{2,1,0:T(2,128)S(1)} %get-tuple-element.12.refs_1_, s32[8,1,2]{2,1,0:T(1,128)S(1)} %get-tuple-element.13.refs_2_, ...), custom_call_target="tpu_custom_call", output_to_operand_aliasing={{0}: (8, {}), {1}: (9, {})} | custom-call | flops 2000000000 | bytes 12582912 | tf_op jit(solution)/shard_map/pallas_call | solution.py:969
  51.6 0.0 copy-done.5
  51.6 96.3 %shard_map.93 = bf16[64,4096]{1,0:T(8,128)(2,1)S(1)} custom-call(bf16[16,2,128,512]{3,2,1,0:T(8,128)(2,1)S(1)} %get-tuple-element.17.o_ref, f32[16,8,128]{2,1,0:T(8,128)S(1)} %get-tuple-element.18.lse_ref, bf16[1024,512]{1,0:T(8,128)(2,1)S(1)} %copy-done.5), custom_call_target="tpu_custom_call" | custom-call | flops 199999995904 | bytes 1048576 | tf_op jit(solution)/shard_map/pallas_call | solution.py:921
  147.9 0.8 copy.15
Async XLA Ops:
  0.0 46.2 %copy-start = (bf16[4096,256]{1,0:T(8,128)(2,1)S(1)}, bf16[4096,256]{1,0:T(8,128)(2,1)}, u32[]{:S(2)}) copy-start(bf16[4096,256]{1,0:T(8,128)(2,1)} %refs_6_.1) | copy-start | bytes 6291460
  0.0 46.2 %copy-start.1 = (bf16[4096,256]{1,0:T(8,128)(2,1)S(1)}, bf16[4096,256]{1,0:T(8,128)(2,1)}, u32[]{:S(2)}) copy-start(bf16[4096,256]{1,0:T(8,128)(2,1)} %refs_7_.1) | copy-start | bytes 6291460
  0.0 46.3 %copy-start.2 = (bf16[256,256]{1,0:T(8,128)(2,1)S(1)}, bf16[256,256]{1,0:T(8,128)(2,1)}, u32[]{:S(2)}) copy-start(bf16[256,256]{1,0:T(8,128)(2,1)} %refs_4_.3) | copy-start | bytes 393220
  0.0 46.3 %copy-start.3 = (bf16[256,256]{1,0:T(8,128)(2,1)S(1)}, bf16[256,256]{1,0:T(8,128)(2,1)}, u32[]{:S(2)}) copy-start(bf16[256,256]{1,0:T(8,128)(2,1)} %refs_5_.3) | copy-start | bytes 393220
  0.0 46.3 %copy-start.4 = (s32[256]{0:T(256)S(1)}, s32[256]{0:T(256)}, u32[]{:S(2)}) copy-start(s32[256]{0:T(256)} %refs_0_.3) | copy-start | bytes 3076
  46.3 5.3 %copy-start.5 = (bf16[1024,512]{1,0:T(8,128)(2,1)S(1)}, bf16[1024,512]{1,0:T(8,128)(2,1)}, u32[]{:S(2)}) copy-start(bf16[1024,512]{1,0:T(8,128)(2,1)} %w_hbm.1) | copy-start | bytes 3145732

commit v4 on v3

--- a/solution.py
+++ b/solution.py
@@ -13,6 +13,7 @@
 BLK = 128
 NEG = -1e30
 SCAN = 4
+AHEAD = 2
 CUTS = 1
 LOG2E = 1.4426950408889634
 MESH = pl.DeviceIdType.MESH
@@ -173,7 +174,7 @@
 def rest_kernel(local_blocks, store_blocks, *refs):
     def row(block, carry):
         first_row = pl.multiple_of(block * BLK, BLK)
-        part_row(block, block, first_row, 1, local_blocks, store_blocks, *refs[:8], *refs[10:])
+        part_row(block, block, first_row, AHEAD, local_blocks, store_blocks, *refs[:8], *refs[10:])
         return carry
 
     lax.fori_loop(0, refs[10].shape[0], row, 0)
@@ -293,40 +294,56 @@
         store_blocks = k_ref.shape[0]
         listed = count_smem[owner, 0, inner]
 
-        def look(i, best):
-            e = degree - SCAN * (i + 1)
-            for u in range(SCAN - 1, -1, -1):
-                spot = slot_ref[near_smem[owner, inner, e + u]] - me * store_blocks
-                kept = ((spot >= 0) & (spot < store_blocks) & (e + u < listed)).astype(jnp.int32)
-                best = best + kept * (spot - best)
-            return best
-
-        return lax.fori_loop(0, degree // SCAN, look, jnp.int32(-1))
-
-    def row_work(owner, inner, spot, mine):
+        def look_past(before):
+            def look(i, best):
+                e = degree - SCAN * (i + 1)
+                for u in range(SCAN - 1, -1, -1):
+                    spot = slot_ref[near_smem[owner, inner, e + u]] - me * store_blocks
+                    kept = (spot >= 0) & (spot < store_blocks) & (e + u < listed)
+                    for other in before:
+                        kept = kept & (spot != other)
+                    best = best + kept.astype(jnp.int32) * (spot - best)
+                return best
+
+            return lax.fori_loop(0, degree // SCAN, look, jnp.int32(-1))
+
+        found = []
+        for _ in range(AHEAD):
+            found.append(look_past(found))
+        return found
+
+    def row_work(owner, inner, spots, mine):
         per_group = H // KVH
-        taken = jnp.maximum(spot, 0)
-        missing = jnp.minimum(spot, 0).astype(jnp.float32) * -NEG
+        taken = [jnp.maximum(spot, 0) for spot in spots]
+        missing = [jnp.minimum(spot, 0).astype(jnp.float32) * -NEG for spot in spots]
         first_row = pl.multiple_of(owner * rows + inner * BLK, BLK)
         for g in range(k_ref.shape[2] // DH):
             cols = slice(g * DH, (g + 1) * DH)
             asked = asked_rows(out_ref, first_row, g, per_group)
-            keys, values = k_ref[taken, :, cols], v_ref[taken, :, cols]
+            keys = [k_ref[i, :, cols] for i in taken]
+            values = [v_ref[i, :, cols] for i in taken]
             if mine:
                 near = pl.ds(pl.multiple_of(inner * BLK, BLK), BLK)
-                keys = jnp.concatenate([sk_ref[near, cols], keys], axis=0)
-                values = jnp.concatenate([sv_ref[near, cols], values], axis=0)
-            s = scores_of(keys, asked)
+                keys = [sk_ref[near, cols]] + keys
+                values = [sv_ref[near, cols]] + values
+            s = scores_of(jnp.concatenate(keys, axis=0), asked)
+            cuts = [s[i * BLK : (i + 1) * BLK] for i in range(len(keys))]
+            for i, lack in enumerate(missing):
+                if mine or i > 0:
+                    at = i + 1 if mine else i
+                    cuts[at] = cuts[at] + lack
             if mine:
-                inside = jnp.where(causal_mask(s.shape[1]), s[:BLK], NEG)
-                s = jnp.concatenate([inside, s[BLK:] + missing], axis=0)
+                cuts[0] = jnp.where(causal_mask(s.shape[1]), cuts[0], NEG)
+            s = jnp.concatenate(cuts, axis=0)
             m = jnp.max(s, axis=0, keepdims=True)
             p = jnp.exp2(s - m)
             total = jnp.sum(p, axis=0, keepdims=True)
             lse = m + jnp.log2(total)
             if not mine:
-                lse = lse + missing
-            write_part(o_ref, lse_ref, owner * pieces + inner, g, weighed(values, p), total, lse)
+                lse = lse + missing[0]
+            write_part(
+                o_ref, lse_ref, owner * pieces + inner, g, weighed(jnp.concatenate(values, axis=0), p), total, lse
+            )
 
     def row_at(way, step, spot):
         return ring_index(place - ways[way] * step, n), piece_of(way, spot)

time: 148 us -> 148 us (level)
  no operation moved by 1% of the time
where the time goes in v4:
time: 148 us
  Pallas kernels  147 us (99%)
    pallas_call x1, Pallas kernels, mixed_from(): call(kernel, 1, [vmem, vmem, anywhere], out, scratch, held)  96.8 us
    pallas_call x1, Pallas kernels, gathered(): pl.pallas_call(functools.partial(gather_kernel, n, pieces, bool(early)),...  45.2 us
    pallas_call x1, Pallas kernels, body(): pl.pallas_call(functools.partial(rest_kernel, local_blocks, store_blocks)...  4.58 us

profile of v4, /device:TPU:3, one launch (start us, length us, event | category | flops | bytes accessed | tf_op | source)
XLA Modules:
  0.0 147.6 jit_solution(3469342881855739295)
XLA Ops:
  0.0 0.0 copy-start
  0.0 0.0 copy-start.1
  0.0 0.0 copy-start.2
  0.0 0.0 copy-start.3
  0.0 0.0 copy-start.4
  0.0 45.2 %shard_map.91 = (bf16[2048,1024]{1,0:T(8,128)(2,1)S(1)}, s32[8,2,64]{2,1,0:T(2,128)S(1)}, s32[8,1,2]{2,1,0:T(1,128)S(1)}, bf16[16,2,128,512]{3,2,1,0:T(8,128)(2,1)S(1)}, f32[16,8,128]{2,1,0:T(8,128)S(1)}) custom-call(bf16[256,1024]{1,0:T(8,128)(2,1)} %refs_0_.2, s32[2,64]{1,0:T(2,128)} %refs_1_.1, s32[1,2]{1,0:T(1,128)} %bitcast.5, s32[256]{0:T(256)} %refs_0_.3, ...), custom_call_target="tpu_custom_call" | custom-call | flops 199999995904 | bytes 1048576 | tf_op jit(solution)/shard_map/pallas_call | solution.py:432
  45.3 0.0 copy-done
  45.3 0.0 copy-done.1
  45.3 0.0 copy-done.2
  45.3 0.0 copy-done.3
  45.3 0.0 copy-done.4
  45.3 0.0 copy-start.5
  45.3 4.6 %shard_map.92 = (bf16[16,2,128,512]{3,2,1,0:T(8,128)(2,1)S(1)}, f32[16,8,128]{2,1,0:T(8,128)S(1)}) custom-call(s32[256]{0:T(256)S(1)} %copy-done.4, s32[8,2,64]{2,1,0:T(2,128)S(1)} %get-tuple-element.12.refs_1_, s32[8,1,2]{2,1,0:T(1,128)S(1)} %get-tuple-element.13.refs_2_, ...), custom_call_target="tpu_custom_call", output_to_operand_aliasing={{0}: (8, {}), {1}: (9, {})} | custom-call | flops 2000000000 | bytes 12582912 | tf_op jit(solution)/shard_map/pallas_call | solution.py:986
  49.9 0.0 copy-done.5
  49.9 96.8 %shard_map.93 = bf16[64,4096]{1,0:T(8,128)(2,1)S(1)} custom-call(bf16[16,2,128,512]{3,2,1,0:T(8,128)(2,1)S(1)} %get-tuple-element.17.o_ref, f32[16,8,128]{2,1,0:T(8,128)S(1)} %get-tuple-element.18.lse_ref, bf16[1024,512]{1,0:T(8,128)(2,1)S(1)} %copy-done.5), custom_call_target="tpu_custom_call" | custom-call | flops 199999995904 | bytes 1048576 | tf_op jit(solution)/shard_map/pallas_call | solution.py:938
  146.8 0.8 copy.15
Async XLA Ops:
  0.0 45.3 %copy-start = (bf16[4096,256]{1,0:T(8,128)(2,1)S(1)}, bf16[4096,256]{1,0:T(8,128)(2,1)}, u32[]{:S(2)}) copy-start(bf16[4096,256]{1,0:T(8,128)(2,1)} %refs_6_.1) | copy-start | bytes 6291460
  0.0 45.3 %copy-start.1 = (bf16[4096,256]{1,0:T(8,128)(2,1)S(1)}, bf16[4096,256]{1,0:T(8,128)(2,1)}, u32[]{:S(2)}) copy-start(bf16[4096,256]{1,0:T(8,128)(2,1)} %refs_7_.1) | copy-start | bytes 6291460
  0.0 45.3 %copy-start.2 = (bf16[256,256]{1,0:T(8,128)(2,1)S(1)}, bf16[256,256]{1,0:T(8,128)(2,1)}, u32[]{:S(2)}) copy-start(bf16[256,256]{1,0:T(8,128)(2,1)} %refs_4_.3) | copy-start | bytes 393220
  0.0 45.3 %copy-start.3 = (bf16[256,256]{1,0:T(8,128)(2,1)S(1)}, bf16[256,256]{1,0:T(8,128)(2,1)}, u32[]{:S(2)}) copy-start(bf16[256,256]{1,0:T(8,128)(2,1)} %refs_5_.3) | copy-start | bytes 393220
  0.0 45.3 %copy-start.4 = (s32[256]{0:T(256)S(1)}, s32[256]{0:T(256)}, u32[]{:S(2)}) copy-start(s32[256]{0:T(256)} %refs_0_.3) | copy-start | bytes 3076
  45.3 4.6 %copy-start.5 = (bf16[1024,512]{1,0:T(8,128)(2,1)S(1)}, bf16[1024,512]{1,0:T(8,128)(2,1)}, u32[]{:S(2)}) copy-start(bf16[1024,512]{1,0:T(8,128)(2,1)} %w_hbm.1) | copy-start | bytes 3145732

commit v5 on v4

--- a/solution.py
+++ b/solution.py
@@ -174,7 +174,12 @@
 def rest_kernel(local_blocks, store_blocks, *refs):
     def row(block, carry):
         first_row = pl.multiple_of(block * BLK, BLK)
-        part_row(block, block, first_row, AHEAD, local_blocks, store_blocks, *refs[:8], *refs[10:])
+        listed = refs[2][lax.div(block, local_blocks), 0, lax.rem(block, local_blocks)]
+
+        @pl.when(listed > AHEAD)
+        def _():
+            part_row(block, block, first_row, AHEAD, local_blocks, store_blocks, *refs[:8], *refs[10:])
+
         return carry
 
     lax.fori_loop(0, refs[10].shape[0], row, 0)

time: 148 us -> 147 us (level)
  no operation moved by 1% of the time
where the time goes in v5:
time: 147 us
  Pallas kernels  146 us (99%)
    pallas_call x1, Pallas kernels, mixed_from(): call(kernel, 1, [vmem, vmem, anywhere], out, scratch, held)  96.8 us
    pallas_call x1, Pallas kernels, gathered(): pl.pallas_call(functools.partial(gather_kernel, n, pieces, bool(early)),...  45.2 us
    pallas_call x1, Pallas kernels, body(): pl.pallas_call(functools.partial(rest_kernel, local_blocks, store_blocks)...  4.3 us

profile of v5, /device:TPU:3, one launch (start us, length us, event | category | flops | bytes accessed | tf_op | source)
XLA Modules:
  0.0 147.3 jit_solution(15640783777484398988)
XLA Ops:
  0.0 0.0 copy-start
  0.0 0.0 copy-start.1
  0.0 0.0 copy-start.2
  0.0 0.0 copy-start.3
  0.0 0.0 copy-start.4
  0.0 45.2 %shard_map.91 = (bf16[2048,1024]{1,0:T(8,128)(2,1)S(1)}, s32[8,2,64]{2,1,0:T(2,128)S(1)}, s32[8,1,2]{2,1,0:T(1,128)S(1)}, bf16[16,2,128,512]{3,2,1,0:T(8,128)(2,1)S(1)}, f32[16,8,128]{2,1,0:T(8,128)S(1)}) custom-call(bf16[256,1024]{1,0:T(8,128)(2,1)} %refs_0_.2, s32[2,64]{1,0:T(2,128)} %refs_1_.1, s32[1,2]{1,0:T(1,128)} %bitcast.5, s32[256]{0:T(256)} %refs_0_.3, ...), custom_call_target="tpu_custom_call" | custom-call | flops 199999995904 | bytes 1048576 | tf_op jit(solution)/shard_map/pallas_call | solution.py:437
  45.3 0.0 copy-done
  45.3 0.0 copy-done.1
  45.3 0.0 copy-done.2
  45.3 0.0 copy-done.3
  45.3 0.0 copy-done.4
  45.3 0.0 copy-start.5
  45.3 4.3 %shard_map.92 = (bf16[16,2,128,512]{3,2,1,0:T(8,128)(2,1)S(1)}, f32[16,8,128]{2,1,0:T(8,128)S(1)}) custom-call(s32[256]{0:T(256)S(1)} %copy-done.4, s32[8,2,64]{2,1,0:T(2,128)S(1)} %get-tuple-element.12.refs_1_, s32[8,1,2]{2,1,0:T(1,128)S(1)} %get-tuple-element.13.refs_2_, ...), custom_call_target="tpu_custom_call", output_to_operand_aliasing={{0}: (8, {}), {1}: (9, {})} | custom-call | flops 2000000000 | bytes 12582912 | tf_op jit(solution)/shard_map/pallas_call | solution.py:991
  49.6 0.0 copy-done.5
  49.7 96.8 %shard_map.93 = bf16[64,4096]{1,0:T(8,128)(2,1)S(1)} custom-call(bf16[16,2,128,512]{3,2,1,0:T(8,128)(2,1)S(1)} %get-tuple-element.17.o_ref, f32[16,8,128]{2,1,0:T(8,128)S(1)} %get-tuple-element.18.lse_ref, bf16[1024,512]{1,0:T(8,128)(2,1)S(1)} %copy-done.5), custom_call_target="tpu_custom_call" | custom-call | flops 199999995904 | bytes 1048576 | tf_op jit(solution)/shard_map/pallas_call | solution.py:943
  146.5 0.8 copy.15
Async XLA Ops:
  0.0 45.3 %copy-start = (bf16[4096,256]{1,0:T(8,128)(2,1)S(1)}, bf16[4096,256]{1,0:T(8,128)(2,1)}, u32[]{:S(2)}) copy-start(bf16[4096,256]{1,0:T(8,128)(2,1)} %refs_6_.1) | copy-start | bytes 6291460
  0.0 45.3 %copy-start.1 = (bf16[4096,256]{1,0:T(8,128)(2,1)S(1)}, bf16[4096,256]{1,0:T(8,128)(2,1)}, u32[]{:S(2)}) copy-start(bf16[4096,256]{1,0:T(8,128)(2,1)} %refs_7_.1) | copy-start | bytes 6291460
  0.0 45.3 %copy-start.2 = (bf16[256,256]{1,0:T(8,128)(2,1)S(1)}, bf16[256,256]{1,0:T(8,128)(2,1)}, u32[]{:S(2)}) copy-start(bf16[256,256]{1,0:T(8,128)(2,1)} %refs_4_.3) | copy-start | bytes 393220
  0.0 45.3 %copy-start.3 = (bf16[256,256]{1,0:T(8,128)(2,1)S(1)}, bf16[256,256]{1,0:T(8,128)(2,1)}, u32[]{:S(2)}) copy-start(bf16[256,256]{1,0:T(8,128)(2,1)} %refs_5_.3) | copy-start | bytes 393220
  0.0 45.3 %copy-start.4 = (s32[256]{0:T(256)S(1)}, s32[256]{0:T(256)}, u32[]{:S(2)}) copy-start(s32[256]{0:T(256)} %refs_0_.3) | copy-start | bytes 3076
  45.3 4.3 %copy-start.5 = (bf16[1024,512]{1,0:T(8,128)(2,1)S(1)}, bf16[1024,512]{1,0:T(8,128)(2,1)}, u32[]{:S(2)}) copy-start(bf16[1024,512]{1,0:T(8,128)(2,1)} %w_hbm.1) | copy-start | bytes 3145732

commit v6 on v5

--- a/solution.py
+++ b/solution.py
@@ -393,7 +393,8 @@
         found = scanned(half, spot)
         for way in range(2):
             copy(way, half - 1, piece_of(way, spot)).wait_recv()
-        arrived(half, spot, found)
+            if early:
+                row_work(*row_at(way, half, spot), found[way], False)
     for one in started:
         one.wait_send()
     for one in table_copies:

time: 147 us -> 148 us (level)
  no operation moved by 1% of the time
where the time goes in v6:
time: 148 us; the launch traced here: 147 us
  Pallas kernels  146 us (99%)
    pallas_call x1, Pallas kernels, mixed_from(): call(kernel, 1, [vmem, vmem, anywhere], out, scratch, held)  96.8 us
    pallas_call x1, Pallas kernels, gathered(): pl.pallas_call(functools.partial(gather_kernel, n, pieces, bool(early)),...  45.4 us
    pallas_call x1, Pallas kernels, body(): pl.pallas_call(functools.partial(rest_kernel, local_blocks, store_blocks)...  4.21 us

profile of v6, /device:TPU:3, one launch (start us, length us, event | category | flops | bytes accessed | tf_op | source)
XLA Modules:
  0.0 147.4 jit_solution(13110083517667222197)
XLA Ops:
  0.0 0.0 copy-start
  0.0 0.0 copy-start.1
  0.0 0.0 copy-start.2
  0.0 0.0 copy-start.3
  0.0 0.0 copy-start.4
  0.0 45.4 %shard_map.91 = (bf16[2048,1024]{1,0:T(8,128)(2,1)S(1)}, s32[8,2,64]{2,1,0:T(2,128)S(1)}, s32[8,1,2]{2,1,0:T(1,128)S(1)}, bf16[16,2,128,512]{3,2,1,0:T(8,128)(2,1)S(1)}, f32[16,8,128]{2,1,0:T(8,128)S(1)}) custom-call(bf16[256,1024]{1,0:T(8,128)(2,1)} %refs_0_.2, s32[2,64]{1,0:T(2,128)} %refs_1_.1, s32[1,2]{1,0:T(1,128)} %bitcast.5, s32[256]{0:T(256)} %refs_0_.3, ...), custom_call_target="tpu_custom_call" | custom-call | flops 199999995904 | bytes 1048576 | tf_op jit(solution)/shard_map/pallas_call | solution.py:438
  45.4 0.0 copy-done
  45.4 0.0 copy-done.1
  45.5 0.0 copy-done.2
  45.5 0.0 copy-done.3
  45.5 0.0 copy-done.4
  45.5 0.0 copy-start.5
  45.5 4.2 %shard_map.92 = (bf16[16,2,128,512]{3,2,1,0:T(8,128)(2,1)S(1)}, f32[16,8,128]{2,1,0:T(8,128)S(1)}) custom-call(s32[256]{0:T(256)S(1)} %copy-done.4, s32[8,2,64]{2,1,0:T(2,128)S(1)} %get-tuple-element.12.refs_1_, s32[8,1,2]{2,1,0:T(1,128)S(1)} %get-tuple-element.13.refs_2_, ...), custom_call_target="tpu_custom_call", output_to_operand_aliasing={{0}: (8, {}), {1}: (9, {})} | custom-call | flops 2000000000 | bytes 12582912 | tf_op jit(solution)/shard_map/pallas_call | solution.py:992
  49.7 0.0 copy-done.5
  49.7 96.8 %shard_map.93 = bf16[64,4096]{1,0:T(8,128)(2,1)S(1)} custom-call(bf16[16,2,128,512]{3,2,1,0:T(8,128)(2,1)S(1)} %get-tuple-element.17.o_ref, f32[16,8,128]{2,1,0:T(8,128)S(1)} %get-tuple-element.18.lse_ref, bf16[1024,512]{1,0:T(8,128)(2,1)S(1)} %copy-done.5), custom_call_target="tpu_custom_call" | custom-call | flops 199999995904 | bytes 1048576 | tf_op jit(solution)/shard_map/pallas_call | solution.py:944
  146.6 0.8 copy.15
Async XLA Ops:
  0.0 45.4 %copy-start = (bf16[4096,256]{1,0:T(8,128)(2,1)S(1)}, bf16[4096,256]{1,0:T(8,128)(2,1)}, u32[]{:S(2)}) copy-start(bf16[4096,256]{1,0:T(8,128)(2,1)} %refs_6_.1) | copy-start | bytes 6291460
  0.0 45.4 %copy-start.1 = (bf16[4096,256]{1,0:T(8,128)(2,1)S(1)}, bf16[4096,256]{1,0:T(8,128)(2,1)}, u32[]{:S(2)}) copy-start(bf16[4096,256]{1,0:T(8,128)(2,1)} %refs_7_.1) | copy-start | bytes 6291460
  0.0 45.5 %copy-start.2 = (bf16[256,256]{1,0:T(8,128)(2,1)S(1)}, bf16[256,256]{1,0:T(8,128)(2,1)}, u32[]{:S(2)}) copy-start(bf16[256,256]{1,0:T(8,128)(2,1)} %refs_4_.3) | copy-start | bytes 393220
  0.0 45.5 %copy-start.3 = (bf16[256,256]{1,0:T(8,128)(2,1)S(1)}, bf16[256,256]{1,0:T(8,128)(2,1)}, u32[]{:S(2)}) copy-start(bf16[256,256]{1,0:T(8,128)(2,1)} %refs_5_.3) | copy-start | bytes 393220
  0.0 45.5 %copy-start.4 = (s32[256]{0:T(256)S(1)}, s32[256]{0:T(256)}, u32[]{:S(2)}) copy-start(s32[256]{0:T(256)} %refs_0_.3) | copy-start | bytes 3076
  45.5 4.2 %copy-start.5 = (bf16[1024,512]{1,0:T(8,128)(2,1)S(1)}, bf16[1024,512]{1,0:T(8,128)(2,1)}, u32[]{:S(2)}) copy-start(bf16[1024,512]{1,0:T(8,128)(2,1)} %w_hbm.1) | copy-start | bytes 3145732
